TPU v7x, 128 devices: a whole 4x4x4 slice. The times are simulated.
128 devices in a mesh: tree: 1, feat: 16 (over z, y), data: 8 (over x, core).
Axes of the slice: x: 4, y: 4, z: 4, core: 2. Of those that a mesh axis runs over, the one named last changes fastest.
Arguments:
- binned: int32 [4096, 128], P(('tree', 'data'), 'feat')
- gradient: float32 [4096], P(('tree', 'data'))
- hessian: float32 [4096], P(('tree', 'data'))
- split_feat: int32 [7, 64], P('tree')
- split_thr: int32 [7, 64], P('tree')
- reg_lambda: float32 [1], replicated
Outputs:
- output 1: float32 [255, 128, 255], P('tree', ('feat', 'data'))
- output 2: float32 [128], P('tree')
All inputs are finite; a program needn't handle non-finite values.
Results may differ from a plain program's by a relative error of at most 0.001.
Values sent between devices are 32-bit elements.
A program may use at most 1 GiB of HBM per device.

v0:
```python
import jax
import jax.numpy as jnp
from jax import lax
from jax.sharding import PartitionSpec as P

NBINS = 256


def bin_width(cells):
    limit = max(1, (1 << 22) // cells)
    width = 1
    while width * 2 <= min(limit, NBINS):
        width = width * 2
    return width


def local_histogram(binned, weights):
    rows, feats = binned.shape
    width = bin_width(rows * feats)
    offsets = jnp.arange(width, dtype=jnp.int32)
    starts = jnp.arange(NBINS // width, dtype=jnp.int32) * width

    def one_block(start):
        indicator = jnp.where(binned[:, :, None] == start + offsets, jnp.float32(1), jnp.float32(0))
        return jnp.einsum('rfb,rk->fbk', indicator, weights, precision=lax.Precision.HIGHEST, preferred_element_type=jnp.float32)

    blocks = lax.map(one_block, starts)
    return jnp.moveaxis(blocks, 0, 1).reshape(feats, NBINS, weights.shape[1])


def node_weights(node, grad_hess, n_nodes):
    member = node[:, None] == jnp.arange(n_nodes, dtype=jnp.int32)[None, :]
    weights = jnp.where(member[:, :, None], grad_hess[:, None, :], jnp.float32(0))
    return weights.reshape(node.shape[0], 2 * n_nodes)


def node_score(pair_sums, reg_value):
    return pair_sums[..., 0] ** 2 / (pair_sums[..., 1] + reg_value)


def split_gains(histogram, reg_value):
    node_sum = jnp.sum(histogram, axis=1, keepdims=True)
    left_sum = jnp.cumsum(histogram, axis=1)[:, :-1]
    right_sum = node_sum - left_sum
    gain = 0.5 * (node_score(left_sum, reg_value) + node_score(right_sum, reg_value) - node_score(node_sum, reg_value))
    return jnp.transpose(gain, (2, 0, 1))


def route_bits(binned, node, feat_row, thr_row, feat_start):
    feats = binned.shape[1]
    local_feat = jnp.take(feat_row, node) - feat_start
    is_chosen = jnp.arange(feats, dtype=jnp.int32)[None, :] == local_feat[:, None]
    picked = jnp.sum(jnp.where(is_chosen, binned, 0), axis=1)
    held = (local_feat >= 0) & (local_feat < feats)
    return jnp.where(held & (picked > jnp.take(thr_row, node)), 1, 0).astype(jnp.int32)


def solution(mesh):
    def per_device(binned, gradient, hessian, split_feat, split_thr, reg_lambda):
        rows, feats = binned.shape
        depth = split_feat.shape[0] + 1
        reg_value = reg_lambda[0]
        grad_hess = jnp.stack([gradient, hessian], axis=1)
        feat_start = lax.axis_index('feat') * feats
        node = jnp.zeros((rows,), jnp.int32)
        pieces = []
        for level in range(depth):
            n_nodes = 2 ** level
            weights = node_weights(node, grad_hess, n_nodes)
            histogram = local_histogram(binned, weights).reshape(feats, NBINS, n_nodes, 2)
            histogram = lax.psum_scatter(histogram, 'data', scatter_dimension=0, tiled=True)
            pieces.append(split_gains(histogram, reg_value))
            if level < depth - 1:
                bits = route_bits(binned, node, split_feat[level, :n_nodes], split_thr[level, :n_nodes], feat_start)
                node = 2 * node + lax.psum(bits, 'feat')
        leaf_sums = lax.psum(jnp.sum(weights, axis=0), 'data').reshape(-1, 2)
        leaf_value = -leaf_sums[:, 0] / (leaf_sums[:, 1] + reg_value)
        return jnp.concatenate(pieces, axis=0), leaf_value

    row_spec = P(('tree', 'data'))
    return jax.shard_map(
        per_device,
        mesh=mesh,
        in_specs=(P(('tree', 'data'), 'feat'), row_spec, row_spec, P('tree', None), P('tree', None), P(None)),
        out_specs=(P('tree', ('feat', 'data'), None), P('tree')),
        check_vma=False,
    )
```

profile of v0, /device:TPU:1, one launch (start us, length us, event | category | flops | bytes accessed | tf_op | source)
XLA Modules:
  0.0 405.7 jit_solution(14091750773091054633)
XLA Ops:
  13.8 14.8 %psum.56 = s32[512]{0:T(512)S(1)} all-reduce(s32[512]{0:T(512)S(1)} %and_select_fusion.5), channel_id=1, replica_groups=mesh['tree'=1,'feat'=16,'data'=8] {'feat'}, use_global_device_ids=true, to_apply=%region_5.7 | all-reduce | flops 512 | bytes 4096 | tf_op jit(solution)/shard_map/psum | solution.py:75
  34.4 7.0 %psum.57 = s32[512]{0:T(512)S(1)} all-reduce(s32[512]{0:T(512)S(1)} %fusion.94), channel_id=1, replica_groups=mesh['tree'=1,'feat'=16,'data'=8] {'feat'}, use_global_device_ids=true, to_apply=%region_11.14 | all-reduce | flops 512 | bytes 4096 | tf_op jit(solution)/shard_map/psum | solution.py:75
  45.4 5.4 %fusion.7 = f32[8,256,4,2]{1,2,3,0:T(4,128)} fusion(s32[512,8]{0,1:T(8,128)} %param.20, f32[4,2,512]{2,1,0:T(2,128)S(1)} %dot_general.65), kind=kOutput, calls=%fused_computation.8 | convolution fusion | flops 102760448 | bytes 98304 | tf_op jit(solution)/shard_map/while/body/eval_jaxpr/rfb,rk->fbk/dot_general | solution.py:25
  54.2 13.3 %psum.58 = s32[512]{0:T(512)S(1)} all-reduce(s32[512]{0:T(512)S(1)} %and_select_fusion.4), channel_id=1, replica_groups=mesh['tree'=1,'feat'=16,'data'=8] {'feat'}, use_global_device_ids=true, to_apply=%region_17.21 | all-reduce | flops 512 | bytes 4096 | tf_op jit(solution)/shard_map/psum | solution.py:75
  68.2 5.0 %select_subtract_fusion.3 = (s32[512]{0:T(512)S(1)}, pred[512]{0:T(512)(128)(4,1)S(1)}, pred[512]{0:T(512)(128)(4,1)S(1)}, pred[512]{0:T(512)(128)(4,1)S(1)}, pr...) fusion(s32[]{:T(128)} %bitcast.76, s32[]{:T(128)} %bitcast.75, ...), kind=kLoop, calls=%fused_computation.206 | loop fusion | flops 12288 | bytes 11812 | tf_op jit(solution)/shard_map/sub | solution.py:51
  73.4 4.7 %fusion.6 = f32[8,256,8,2]{1,2,3,0:T(8,128)} fusion(s32[512,8]{0,1:T(8,128)S(1)} %copy-done, f32[8,2,512]{2,1,0:T(2,128)S(1)} %dot_general.68), kind=kOutput, calls=%fused_computation.7 | convolution fusion | flops 203423744 | bytes 180224 | tf_op jit(solution)/shard_map/while/body/eval_jaxpr/rfb,rk->fbk/dot_general | solution.py:25
  78.9 5.1 %and_select_fusion.3 = s32[512]{0:T(512)S(1)} fusion(s32[512]{0:T(512)S(1)} %get-tuple-element.257, s32[512]{0:T(512)S(1)} %select_reduce_fusion.3, pred[512]{0:T(512)(128)(4,1)S(1)} %get-tuple-element.264, pred[512]{0:T(512)(128)(4,1)S(1)} %get-tuple-element.263, pred[512]{0:T(512)(128)(4,1)S(1)} %get-tuple-element.262, ...), kind=kLoop, calls=%fused_computation.229 | loop fusion | flops 10240 | bytes 11808 | tf_op jit(solution)/shard_map/jit(_where)/select_n | solution.py:55
  84.0 7.2 %psum.59 = s32[512]{0:T(512)S(1)} all-reduce(s32[512]{0:T(512)S(1)} %and_select_fusion.3), channel_id=1, replica_groups=mesh['tree'=1,'feat'=16,'data'=8] {'feat'}, use_global_device_ids=true, to_apply=%region_23.28 | all-reduce | flops 512 | bytes 4096 | tf_op jit(solution)/shard_map/psum | solution.py:75
  92.0 10.0 %select_subtract_fusion.2 = (s32[512]{0:T(512)S(1)}, pred[512]{0:T(512)(128)(4,1)S(1)}, pred[512]{0:T(512)(128)(4,1)S(1)}, pred[512]{0:T(512)(128)(4,1)S(1)}, pr...) fusion(s32[]{:T(128)} %bitcast.114, ...), kind=kLoop, calls=%fused_computation.204 | loop fusion | flops 20480 | bytes 15940 | tf_op jit(solution)/shard_map/sub | solution.py:51
  102.1 5.1 %fusion.5 = f32[8,256,16,2]{1,2,3,0:T(8,128)} fusion(s32[512,8]{0,1:T(8,128)S(1)} %copy-done, f32[16,2,512]{2,1,0:T(2,128)S(1)} %dot_general.71), kind=kOutput, calls=%fused_computation.6 | convolution fusion | flops 404750336 | bytes 344064 | tf_op jit(solution)/shard_map/while/body/eval_jaxpr/rfb,rk->fbk/dot_general | solution.py:25
  109.5 9.9 %and_select_fusion.2 = s32[512]{0:T(512)S(1)} fusion(s32[512]{0:T(512)S(1)} %get-tuple-element.240, s32[512]{0:T(512)S(1)} %select_reduce_fusion.2, pred[512]{0:T(512)(128)(4,1)S(1)} %get-tuple-element.255, pred[512]{0:T(512)(128)(4,1)S(1)} %get-tuple-element.254, pred[512]{0:T(512)(128)(4,1)S(1)} %get-tuple-element.253, ...), kind=kLoop, calls=%fused_computation.228 | loop fusion | flops 14336 | bytes 15936 | tf_op jit(solution)/shard_map/jit(_where)/select_n | solution.py:55
  119.4 13.4 %psum.60 = s32[512]{0:T(512)S(1)} all-reduce(s32[512]{0:T(512)S(1)} %and_select_fusion.2), channel_id=1, replica_groups=mesh['tree'=1,'feat'=16,'data'=8] {'feat'}, use_global_device_ids=true, to_apply=%region_29.35 | all-reduce | flops 512 | bytes 4096 | tf_op jit(solution)/shard_map/psum | solution.py:75
  132.8 20.0 %select_subtract_fusion.1 = (s32[512]{0:T(512)S(1)}, pred[512]{0:T(512)(128)(4,1)S(1)}, pred[512]{0:T(512)(128)(4,1)S(1)}, pred[512]{0:T(512)(128)(4,1)S(1)}, pr...) fusion(s32[]{:T(128)} %bitcast.176, ...), kind=kLoop, calls=%fused_computation.202 | loop fusion | flops 36864 | bytes 24196 | tf_op jit(solution)/shard_map/sub | solution.py:51
  153.0 5.4 %fusion.4 = f32[8,256,32,2]{1,2,3,0:T(8,128)} fusion(s32[512,8]{0,1:T(8,128)S(1)} %copy-done, f32[32,2,512]{2,1,0:T(2,128)S(1)} %dot_general.74), kind=kOutput, calls=%fused_computation.5 | convolution fusion | flops 807403520 | bytes 671744 | tf_op jit(solution)/shard_map/while/body/eval_jaxpr/rfb,rk->fbk/dot_general | solution.py:25
  162.2 19.8 %and_select_fusion.1 = s32[512]{0:T(512)S(1)} fusion(s32[512]{0:T(512)S(1)} %get-tuple-element.207, s32[512]{0:T(512)S(1)} %select_reduce_fusion.1, pred[512]{0:T(512)(128)(4,1)S(1)} %get-tuple-element.238, pred[512]{0:T(512)(128)(4,1)S(1)} %get-tuple-element.237, pred[512]{0:T(512)(128)(4,1)S(1)} %get-tuple-element.236, ...), kind=kLoop, calls=%fused_computation.227 | loop fusion | flops 22528 | bytes 24192 | tf_op jit(solution)/shard_map/jit(_where)/select_n | solution.py:55
  182.0 7.8 %psum.61 = s32[512]{0:T(512)S(1)} all-reduce(s32[512]{0:T(512)S(1)} %and_select_fusion.1), channel_id=1, replica_groups=mesh['tree'=1,'feat'=16,'data'=8] {'feat'}, use_global_device_ids=true, to_apply=%region_35.42 | all-reduce | flops 512 | bytes 4096 | tf_op jit(solution)/shard_map/psum | solution.py:75
  190.5 40.1 %select_subtract_fusion = (s32[512]{0:T(512)S(1)}, pred[512]{0:T(512)(128)(4,1)S(1)}, pred[512]{0:T(512)(128)(4,1)S(1)}, pred[512]{0:T(512)(128)(4,1)S(1)}, pred...) fusion(s32[]{:T(128)} %bitcast.287, ...), kind=kLoop, calls=%fused_computation.200 | loop fusion | flops 69632 | bytes 40708 | tf_op jit(solution)/shard_map/sub | solution.py:51
  231.2 5.8 %fusion.3 = f32[8,256,64,2]{1,2,3,0:T(8,128)} fusion(s32[512,8]{0,1:T(8,128)S(1)} %copy-done, f32[64,2,512]{2,1,0:T(2,128)S(1)} %dot_general.77), kind=kOutput, calls=%fused_computation.4 | convolution fusion | flops 1612709888 | bytes 1327104 | tf_op jit(solution)/shard_map/while/body/eval_jaxpr/rfb,rk->fbk/dot_general | solution.py:25
  240.0 40.1 %and_select_fusion = s32[512]{0:T(512)S(1)} fusion(s32[512]{0:T(512)S(1)} %get-tuple-element.122, s32[512]{0:T(512)S(1)} %select_reduce_fusion, pred[512]{0:T(512)(128)(4,1)S(1)} %get-tuple-element.205, pred[512]{0:T(512)(128)(4,1)S(1)} %get-tuple-element.204, pred[512]{0:T(512)(128)(4,1)S(1)} %get-tuple-element.203, ...), kind=kLoop, calls=%fused_computation.226 | loop fusion | flops 38912 | bytes 40704 | tf_op jit(solution)/shard_map/jit(_where)/select_n | solution.py:55
  280.0 20.9 %psum.62 = s32[512]{0:T(512)S(1)} all-reduce(s32[512]{0:T(512)S(1)} %and_select_fusion), channel_id=1, replica_groups=mesh['tree'=1,'feat'=16,'data'=8] {'feat'}, use_global_device_ids=true, to_apply=%region_41.49 | all-reduce | flops 512 | bytes 4096 | tf_op jit(solution)/shard_map/psum | solution.py:75
  302.2 5.1 %fusion.2 = f32[8,256,128,2]{2,1,3,0:T(8,128)} fusion(s32[512,8]{0,1:T(8,128)S(1)} %copy-done, f32[128,2,512]{2,1,0:T(2,128)S(1)} %dot_general.80), kind=kOutput, calls=%fused_computation.3 | convolution fusion | flops 3223322624 | bytes 2637824 | tf_op jit(solution)/shard_map/while/body/eval_jaxpr/rfb,rk->fbk/dot_general | solution.py:25
  308.0 4.1 %fusion.33 = f32[8,256,1,2]{1,3,0,2:T(2,128)S(1)} fusion(s32[512,8]{0,1:T(8,128)S(1)} %copy-done, f32[512,1]{0,1:T(1,128)S(1)} %bitcast.582, f32[512,1]{0,1:T(1,128)S(1)} %bitcast.584), kind=kOutput, calls=%fused_computation.35 | convolution fusion | flops 27264000 | bytes 36864 | tf_op jit(solution)/shard_map/while/body/eval_jaxpr/rfb,rk->fbk/dot_general | solution.py:25
  312.1 4.3 %fusion.8 = f32[8,256,2,2]{1,3,2,0:T(2,128)S(1)} fusion(f32[2,2,512,1]{2,1,0,3:T(2,128)S(1)} %reshape.2167, s32[512,8]{0,1:T(8,128)S(1)} %copy-done), kind=kOutput, calls=%fused_computation.9 | convolution fusion | flops 52428800 | bytes 57344 | tf_op jit(solution)/shard_map/while/body/eval_jaxpr/rfb,rk->fbk/dot_general | solution.py:25
  317.0 48.8 %all-reduce.3 = (f32[8,256,1,2]{1,3,0,2:T(2,128)S(1)}, f32[8,256,2,2]{1,3,2,0:T(2,128)S(1)}, f32[128,2]{1,0:T(8,128)S(1)}) all-reduce(f32[8,256,1,2]{1,3,0,2:T(2,128)S(1)} %fusion.33, f32[8,256,2,2]{1,3,2,0:T(2,128)S(1)} %fusion.8, f32[128,2]{1,0:T(8,128)S(1)} %get-tuple-element.274), channel_id=2, replica_groups=mesh['tree'=1,'feat'=16,'data'=8] {'data'}, use_global_device_ids=true, to_apply=%region_0.1.clone | all-reduce | flops 12544 | bytes 100352
  (218 shorter events, 64.0 us)
Async XLA Ops:
  7.2 43.8 %copy-start.3 = (s32[7,64]{1,0:T(8,128)S(1)}, s32[7,64]{1,0:T(8,128)}, u32[]{:S(2)}) copy-start(s32[7,64]{1,0:T(8,128)} %param.23) | copy-start | bytes 5380
  7.2 43.7 %copy-start.4 = (s32[7,64]{1,0:T(8,128)S(1)}, s32[7,64]{1,0:T(8,128)}, u32[]{:S(2)}) copy-start(s32[7,64]{1,0:T(8,128)} %param.24) | copy-start | bytes 5380
  7.2 43.8 %copy-start = (s32[512,8]{0,1:T(8,128)S(1)}, s32[512,8]{0,1:T(8,128)}, u32[]{:S(2)}) copy-start(s32[512,8]{0,1:T(8,128)} %param.20) | copy-start | bytes 49156
  7.2 367.7 %all-reduce.6.cloned.1.call-start = ((), (), s32[]{:S(2)}) async-start(), calls=%async_computation.10 | async-start | bytes 131072
  50.8 328.7 %reduce-scatter.7.cloned.1.call-start = ((), (), s32[]{:S(2)}) async-start(), calls=%async_computation.5 | async-start | bytes 147456 | tf_op jit(solution)/shard_map/reduce_scatter | solution.py:71
  78.1 305.0 %reduce-scatter.9.cloned.1.call-start = ((), (), s32[]{:S(2)}) async-start(), calls=%async_computation.6 | async-start | bytes 294912 | tf_op jit(solution)/shard_map/reduce_scatter | solution.py:71
  107.3 279.4 %reduce-scatter.11.cloned.1.call-start = ((), (), s32[]{:S(2)}) async-start(), calls=%async_computation.7 | async-start | bytes 589824 | tf_op jit(solution)/shard_map/reduce_scatter | solution.py:71
  158.5 232.1 %reduce-scatter.13.cloned.1.call-start = ((), (), s32[]{:S(2)}) async-start(), calls=%async_computation.8 | async-start | bytes 1179648 | tf_op jit(solution)/shard_map/reduce_scatter | solution.py:71
  237.0 158.0 %reduce-scatter.15.cloned.1.call-start = ((), (), s32[]{:S(2)}) async-start(), calls=%async_computation.9 | async-start | bytes 2359296 | tf_op jit(solution)/shard_map/reduce_scatter | solution.py:71
  307.3 0.7 copy-start.1
  307.3 0.7 copy-start.2
  312.1 4.3 %copy-start.5 = (u32[128]{0:T(128)S(1)}, u32[128]{0:T(128)}, u32[]{:S(2)}) copy-start(u32[128]{0:T(128)} %constant.710) | copy-start | bytes 1540
Sparse Core Ops, SparseCore 0:
  51.0 66.6 all-reduce.5
  120.6 29.3 reduce-scatter.6
  152.3 29.7 reduce-scatter.8
  184.3 30.0 reduce-scatter.10
  237.2 52.8 reduce-scatter.12
  307.5 54.2 reduce-scatter.14
where the time goes:
time: 414 us; the launch traced here: 406 us
  other arithmetic  185 us (45%)
  blocking collectives  133 us (32%)
  matrix products  40 us (10%)
  local copies, waits for them, and re-layouts  28.9 us (7%)
  between operations  18.5 us (4%)
    psum x7, blocking collectives, per_device(): node = 2 * node + lax.psum(bits, 'feat')  84.5 us
    select_n x7, other arithmetic, route_bits(): jnp.where(held & (picked > jnp.take(thr_row, node)), 1, 0).astype(jnp.int32)  80.6 us
    sub x6, other arithmetic, route_bits(): local_feat = jnp.take(feat_row, node) - feat_start  79 us
    unnamed x1, blocking collectives  48.8 us
    dot_general x8, matrix products, one_block(): jnp.einsum('rfb,rk->fbk', indicator, weights, precision=lax.Precision.HIG...  40 us
    another operation x24, other arithmetic  12.3 us
  transfers between devices with their start and end apart: 6, of which 0 were waited for; matrix products, arithmetic and copies ran while one was open for 56% of the time, Pallas kernels for 0%

commit v1 on v0

v1 whole, which is shorter than its diff:
```python
import functools

import jax
import jax.numpy as jnp
from jax import lax
from jax.experimental import pallas as pl
from jax.experimental.pallas import tpu as pltpu
from jax.sharding import PartitionSpec as P

NBINS = 256
SIDE = 4
NF = SIDE * SIDE
ND = 8
CHUNK = 512
LEAVES = 128
MESH = pl.DeviceIdType.MESH


def split3(value):
    first = value.astype(jnp.bfloat16)
    rest = value - first.astype(jnp.float32)
    second = rest.astype(jnp.bfloat16)
    third = (rest - second.astype(jnp.float32)).astype(jnp.bfloat16)
    return first, second, third


def iota(shape, dim):
    return lax.broadcasted_iota(jnp.int32, shape, dim)


def contract_lanes(left, right):
    return lax.dot_general(left, right, (((1,), (1,)), ((), ())), preferred_element_type=jnp.float32)


def node_tables(feat_tbl, thr_tbl):
    lane = iota((8, 128), 1)
    feat_row = jnp.zeros((1, 128), jnp.int32)
    thr_row = jnp.zeros((1, 128), jnp.int32)
    for level in range(7):
        here = (lane >= 2 ** level) & (lane < 2 ** (level + 1))
        feat_row = feat_row + jnp.where(here, pltpu.roll(feat_tbl, 2 ** level, 1), 0)[level:level + 1]
        thr_row = thr_row + jnp.where(here, pltpu.roll(thr_tbl, 2 ** level, 1), 0)[level:level + 1]
    one, zero = jnp.float32(1), jnp.float32(0)
    by_feat = jnp.where(feat_row == iota((128, 128), 0), one, zero).astype(jnp.bfloat16)
    by_thr = jnp.broadcast_to(thr_row.astype(jnp.float32), (128, 128)).astype(jnp.bfloat16)
    position = iota((128, 128), 0)
    reverse = jnp.zeros((128, 128), jnp.int32)
    for bit in range(7):
        reverse = reverse | (((position >> bit) & 1) << (6 - bit))
    heap = jnp.zeros((128, 128), jnp.int32)
    for level in range(7):
        heap = jnp.where(position >= 2 ** level, 2 ** level + (reverse >> (7 - level)), heap)
    order = jnp.where(heap == iota((128, 128), 1), one, zero).astype(jnp.bfloat16)
    return contract_lanes(order, by_feat).astype(jnp.bfloat16), contract_lanes(order, by_thr)


def route(values, select, threshold):
    picked = jnp.dot(select, values, preferred_element_type=jnp.float32)
    limit = jnp.concatenate([threshold] * (values.shape[1] // 128), axis=1)
    right = picked > limit
    leaf = jnp.where(right[64:128], 1, 0)
    for level in range(5, -1, -1):
        n = 2 ** level
        leaf = jnp.where(right[n:2 * n], leaf[n:] + 2 ** (6 - level), leaf[:n])
    return leaf


def exchange_kernel(bin_hbm, grad_hbm, hess_hbm, feat_hbm, thr_hbm,
                    cols, grads, hesses, leaves,
                    values, feat_in, thr_in, feat_tbl, thr_tbl, local_sem,
                    feat_send, feat_recv, data_send, data_recv, leaf_send, leaf_recv):
    f, d = lax.axis_index('feat'), lax.axis_index('data')
    z, y = f // SIDE, f % SIDE
    shifts = [(a, b) for a in range(SIDE) for b in range(SIDE) if a or b]
    distance = lambda s: min(s[0], SIDE - s[0]) + min(s[1], SIDE - s[1])
    shifts.sort(key=lambda s: -distance(s))
    feat_peers = [((z + a) % SIDE) * SIDE + (y + b) % SIDE for a, b in shifts]
    data_peers = [(d + k) % ND for k in range(1, ND)]

    local = [
        pltpu.make_async_copy(bin_hbm, values.at[f], local_sem.at[0]),
        pltpu.make_async_copy(bin_hbm, cols.at[d], local_sem.at[1]),
        pltpu.make_async_copy(grad_hbm, grads.at[d], local_sem.at[2]),
        pltpu.make_async_copy(hess_hbm, hesses.at[d], local_sem.at[3]),
        pltpu.make_async_copy(feat_hbm, feat_in, local_sem.at[4]),
        pltpu.make_async_copy(thr_hbm, thr_in, local_sem.at[5]),
    ]
    barrier = pltpu.get_barrier_semaphore()
    for peer in feat_peers:
        pl.semaphore_signal(barrier, inc=1, device_id={'feat': peer}, device_id_type=MESH)
    for peer in data_peers:
        pl.semaphore_signal(barrier, inc=1, device_id={'data': peer}, device_id_type=MESH)
    for copy in local:
        copy.start()
    for copy in local:
        copy.wait()
    pl.semaphore_wait(barrier, NF - 1 + ND - 1)

    feat_copies = []
    for k, peer in enumerate(feat_peers):
        copy = pltpu.make_async_remote_copy(
            src_ref=values.at[f], dst_ref=values.at[f], send_sem=feat_send.at[k], recv_sem=feat_recv.at[k],
            device_id={'feat': peer}, device_id_type=MESH)
        copy.start()
        feat_copies.append(copy)
    data_copies = []
    for k, peer in enumerate(data_peers):
        for part, ref in enumerate((cols, grads, hesses)):
            copy = pltpu.make_async_remote_copy(
                src_ref=ref.at[d], dst_ref=ref.at[d], send_sem=data_send.at[part, k], recv_sem=data_recv.at[part, k],
                device_id={'data': peer}, device_id_type=MESH)
            copy.start()
            data_copies.append(copy)

    feat_tbl[...] = jnp.zeros_like(feat_tbl)
    thr_tbl[...] = jnp.zeros_like(thr_tbl)
    feat_tbl[0:7, 0:64] = feat_in[...]
    thr_tbl[0:7, 0:64] = thr_in[...]
    select, threshold = node_tables(feat_tbl[...], thr_tbl[...])
    for copy in feat_copies:
        copy.wait_recv()
    table = values[...].reshape(NF * 8, CHUNK).astype(jnp.float32).astype(jnp.bfloat16)
    leaves[d] = route(table, select, threshold)
    leaf_copies = []
    for k, peer in enumerate(data_peers):
        copy = pltpu.make_async_remote_copy(
            src_ref=leaves.at[d], dst_ref=leaves.at[d], send_sem=leaf_send.at[k], recv_sem=leaf_recv.at[k],
            device_id={'data': peer}, device_id_type=MESH)
        copy.start()
        leaf_copies.append(copy)
    for copy in feat_copies:
        copy.wait_send()
    for copy in data_copies + leaf_copies:
        copy.wait()


def gain_kernel(reg_ref, cols, grads, hesses, leaves, gain_ref, leaf_ref, heap_g, heap_h):
    mine = lax.axis_index('data')
    reg = reg_ref[0]
    zero = jnp.float32(0)
    total = jnp.zeros((2 * LEAVES, NBINS), jnp.float32)
    for d in range(ND):
        column = cols[d, pl.ds(mine, 1), :]
        below = jnp.where(column <= iota((NBINS, CHUNK), 0), jnp.float32(1), zero).astype(jnp.bfloat16)
        member = leaves[d] == iota((LEAVES, CHUNK), 0)
        for g, h in zip(split3(grads[d]), split3(hesses[d])):
            weights = jnp.concatenate([
                jnp.where(member, g.astype(jnp.float32), zero),
                jnp.where(member, h.astype(jnp.float32), zero)], axis=0).astype(jnp.bfloat16)
            total = total + contract_lanes(weights, below)
    for half in range(2):
        lanes = slice(128 * half, 128 * half + 128)
        heap_g[half, 128:256, :] = total[:LEAVES, lanes]
        heap_h[half, 128:256, :] = total[LEAVES:, lanes]
    for level in range(6, -1, -1):
        n = 2 ** level
        for half in range(2):
            for heap in (heap_g, heap_h):
                left = heap[half, pl.ds(2 * n, n, stride=2), :]
                right = heap[half, pl.ds(2 * n + 1, n, stride=2), :]
                heap[half, n:2 * n, :] = left + right

    def score(g, h):
        return g * g / (h + reg)

    for start in range(0, 255, 8):
        n = min(8, 255 - start)
        rows = pl.ds(1 + start, n)
        all_g = heap_g[1, rows, 127:128]
        all_h = heap_h[1, rows, 127:128]
        whole = score(all_g, all_h)
        for half in range(2):
            left_g, left_h = heap_g[half, rows, :], heap_h[half, rows, :]
            gain = 0.5 * (score(left_g, left_h) + score(all_g - left_g, all_h - left_h) - whole)
            wide = 128 - half
            gain_ref[pl.ds(start, n), 0, pl.ds(128 * half, wide)] = gain[:, :wide]
    value = -heap_g[1, 128:256, :] / (heap_h[1, 128:256, :] + reg)
    leaf_ref[...] = value.T[127:128, :]


def solution(mesh):
    def per_device(binned, gradient, hessian, split_feat, split_thr, reg_lambda):
        any_spec = pl.BlockSpec(memory_space=pl.ANY)
        vmem = pl.BlockSpec(memory_space=pltpu.VMEM)
        dma = pltpu.SemaphoreType.DMA
        cols, grads, hesses, leaves = pl.pallas_call(
            exchange_kernel,
            out_shape=[
                jax.ShapeDtypeStruct((ND, 8, CHUNK), jnp.int32),
                jax.ShapeDtypeStruct((ND, 1, CHUNK), jnp.float32),
                jax.ShapeDtypeStruct((ND, 1, CHUNK), jnp.float32),
                jax.ShapeDtypeStruct((ND, 1, CHUNK), jnp.int32),
            ],
            in_specs=[any_spec] * 5,
            out_specs=[vmem] * 4,
            scratch_shapes=[
                pltpu.VMEM((NF, 8, CHUNK), jnp.int32),
                pltpu.VMEM((7, 64), jnp.int32),
                pltpu.VMEM((7, 64), jnp.int32),
                pltpu.VMEM((8, 128), jnp.int32),
                pltpu.VMEM((8, 128), jnp.int32),
                dma((6,)),
                dma((NF - 1,)), dma((NF - 1,)),
                dma((3, ND - 1)), dma((3, ND - 1)),
                dma((ND - 1,)), dma((ND - 1,)),
            ],
            compiler_params=pltpu.CompilerParams(collective_id=0, has_side_effects=True),
            name='exchange',
        )(binned.T, gradient.reshape(1, CHUNK), hessian.reshape(1, CHUNK), split_feat, split_thr)
        gain, leaf_value = pl.pallas_call(
            gain_kernel,
            out_shape=[
                jax.ShapeDtypeStruct((255, 1, 255), jnp.float32),
                jax.ShapeDtypeStruct((1, LEAVES), jnp.float32),
            ],
            in_specs=[pl.BlockSpec(memory_space=pltpu.SMEM)] + [vmem] * 4,
            out_specs=[vmem] * 2,
            scratch_shapes=[pltpu.VMEM((2, 256, 128), jnp.float32), pltpu.VMEM((2, 256, 128), jnp.float32)],
            name='gains',
        )(reg_lambda, cols, grads, hesses, leaves)
        return gain, leaf_value.reshape(LEAVES)

    row_spec = P(('tree', 'data'))
    return jax.shard_map(
        per_device,
        mesh=mesh,
        in_specs=(P(('tree', 'data'), 'feat'), row_spec, row_spec, P('tree', None), P('tree', None), P(None)),
        out_specs=(P('tree', ('feat', 'data'), None), P('tree')),
        check_vma=False,
    )
```

time: 414 us -> 24.3 us (0.06); the launches traced: 406 us -> 24.1 us
  other arithmetic: 185 us -> 0 us
  blocking collectives: 133 us -> 0 us
  matrix products: 40 us -> 0 us
  local copies, waits for them, and re-layouts: 28.9 us -> 0 us
  Pallas kernels: 0 us -> 22.8 us
  between operations: 18.5 us -> 1.29 us
    psum x7 -> x0, blocking collectives: 84.5 us -> none  [per_device(): node = 2 * node + lax.psum(bits, 'feat')]
    select_n x14 -> x0, other arithmetic: 81.4 us -> none  [the longest x7 80.6 us: route_bits(): jnp.where(held & (picked > jnp.take(thr_row, node)), 1, 0).astype(jnp.int32)]
    sub x14 -> x0, other arithmetic: 79.7 us -> none  [the longest x6 79 us: route_bits(): local_feat = jnp.take(feat_row, node) - feat_start]
    unnamed x1 -> x0, blocking collectives: 48.8 us -> none
    dot_general x8 -> x0, matrix products: 40 us -> none  [one_block(): jnp.einsum('rfb,rk->fbk', indicator, weights, precision=lax.Precision.HIG...]
    pallas_call x0 -> x2, Pallas kernels: none -> 22.8 us  [the longest x1 19 us: per_device(): pl.pallas_call(exchange_kernel, out_shape=[jax.ShapeDtypeStruct((ND, 8, C...]
    gather x20 -> x0, local copies, waits for them, and re-layouts: 14 us -> none  [the longest x10 6.98 us: route_bits(): jnp.take(thr_row, node)]
    another operation x25 -> x0, other arithmetic: 13 us -> none
  transfers between devices with their start and end apart: 6 -> 0, of which waited for: 0 -> 0; matrix products, arithmetic and copies ran while one was open for 56% -> 0% of each run, Pallas kernels for 0% -> 0%
where the time goes in v1:
time: 24.3 us; the launch traced here: 24.1 us
  Pallas kernels  22.8 us (94%)
  between operations  1.29 us (5%)
    pallas_call x1, Pallas kernels, per_device(): pl.pallas_call(exchange_kernel, out_shape=[jax.ShapeDtypeStruct((ND, 8, C...  19 us
    pallas_call x1, Pallas kernels, per_device(): pl.pallas_call(gain_kernel, out_shape=[jax.ShapeDtypeStruct((255, 1, 255)...  3.85 us

profile of v1, /device:TPU:1, one launch (start us, length us, event | category | flops | bytes accessed | tf_op | source)
XLA Modules:
  0.0 24.1 jit_solution(17100698311743459103)
XLA Ops:
  1.3 19.0 %exchange.1 = (s32[8,8,512]{2,1,0:T(8,128)}, f32[8,1,512]{2,1,0:T(1,128)}, f32[8,1,512]{2,1,0:T(1,128)}, s32[8,1,512]{2,1,0:T(1,128)}) custom-call(s32[8,512]{1,0:T(8,128)} %bitcast.4, f32[1,512]{1,0:T(1,128)} %bitcast.5, f32[1,512]{1,0:T(1,128)} %bitcast.6, s32[7,64]{1,0:T(8,128)} %feat_hbm.1, s32[7,64]{1,0:T(8,128)} %thr_hbm.1), custom_call_target="tpu_custom_call" | custom-call | tf_op jit(solution)/shard_map/exchange/pallas_call | solution.py:186
  20.3 3.9 %gains.1 = (f32[255,1,255]{2,1,0:T(1,128)}, f32[1,128]{1,0:T(1,128)}) custom-call(f32[1]{0:T(128)S(6)} %copy.8.reg_ref, s32[8,8,512]{2,1,0:T(8,128)} %get-tuple-element.8.cols, f32[8,1,512]{2,1,0:T(1,128)} %get-tuple-element.9.grads, f32[8,1,512]{2,1,0:T(1,128)} %get-tuple-element.10.hesses, s32[8,1,512]{2,1,0:T(1,128)} %get-tuple-element.11.leaves), custom_call_target="tpu_custom_call" | custom-call | tf_op jit(solution)/shard_map/gains/pallas_call | solution.py:210

commit v2 on v1

v2 whole, which is shorter than its diff:
```python
import jax
import jax.numpy as jnp
from jax import lax
from jax.experimental import pallas as pl
from jax.experimental.pallas import tpu as pltpu
from jax.sharding import PartitionSpec as P

NBINS = 256
SIDE = 4
NF = SIDE * SIDE
ND = 8
CHUNK = 512
LEAVES = 128
FEAT_ORDER = sorted(range(NF), key=lambda f: min(f // SIDE, SIDE - f // SIDE) + min(f % SIDE, SIDE - f % SIDE))
MESH = pl.DeviceIdType.MESH


def split3(value):
    first = value.astype(jnp.bfloat16)
    rest = value - first.astype(jnp.float32)
    second = rest.astype(jnp.bfloat16)
    third = (rest - second.astype(jnp.float32)).astype(jnp.bfloat16)
    return first, second, third


def iota(shape, dim):
    return lax.broadcasted_iota(jnp.int32, shape, dim)


def contract_lanes(left, right):
    return lax.dot_general(left, right, (((1,), (1,)), ((), ())), preferred_element_type=jnp.float32)


def node_tables(feat_tbl, thr_tbl):
    lane = iota((8, 128), 1)
    feat_row = jnp.zeros((1, 128), jnp.int32)
    thr_row = jnp.zeros((1, 128), jnp.int32)
    for level in range(7):
        here = (lane >= 2 ** level) & (lane < 2 ** (level + 1))
        feat_row = feat_row + jnp.where(here, pltpu.roll(feat_tbl, 2 ** level, 1), 0)[level:level + 1]
        thr_row = thr_row + jnp.where(here, pltpu.roll(thr_tbl, 2 ** level, 1), 0)[level:level + 1]
    one, zero = jnp.float32(1), jnp.float32(0)
    by_feat = jnp.where(feat_row == iota((128, 128), 0), one, zero).astype(jnp.bfloat16)
    by_thr = jnp.broadcast_to(thr_row.astype(jnp.float32), (128, 128)).astype(jnp.bfloat16)
    position = iota((128, 128), 0)
    reverse = jnp.zeros((128, 128), jnp.int32)
    for bit in range(7):
        reverse = reverse | (((position >> bit) & 1) << (6 - bit))
    heap = jnp.zeros((128, 128), jnp.int32)
    for level in range(7):
        heap = jnp.where(position >= 2 ** level, 2 ** level + (reverse >> (7 - level)), heap)
    order = jnp.where(heap == iota((128, 128), 1), one, zero).astype(jnp.bfloat16)
    return contract_lanes(order, by_feat).astype(jnp.bfloat16), contract_lanes(order, by_thr)


def route(values, select, threshold):
    picked = jnp.dot(select, values, preferred_element_type=jnp.float32)
    limit = jnp.concatenate([threshold] * (values.shape[1] // 128), axis=1)
    right = picked > limit
    leaf = jnp.where(right[64:128], 1, 0)
    for level in range(5, -1, -1):
        n = 2 ** level
        leaf = jnp.where(right[n:2 * n], leaf[n:] + 2 ** (6 - level), leaf[:n])
    return leaf


def exchange_kernel(bin_hbm, grad_hbm, hess_hbm, feat_hbm, thr_hbm, reg_hbm, sums, leaf_sums, reg_row,
                    values, parcels, rows, leaves, below, own_bins, own_grad, own_hess, reg_in, feat_in, thr_in, feat_tbl, thr_tbl,
                    local_sem, feat_send, feat_recv, data_send, data_recv, leaf_send, leaf_recv):
    f, d = lax.axis_index('feat'), lax.axis_index('data')
    x, core = d // 2, d % 2
    near = x + 1 - 2 * (x % 2)
    lines = [near, SIDE - 1 - x, (x + 2) % SIDE]
    data_peers = [2 * x + 1 - core] + [2 * line + c for c in (1, 0) for line in lines]

    own = pltpu.make_async_copy(bin_hbm, values.at[f], feat_recv)
    local = [
        pltpu.make_async_copy(bin_hbm, own_bins, local_sem.at[0]),
        pltpu.make_async_copy(grad_hbm, own_grad, local_sem.at[1]),
        pltpu.make_async_copy(hess_hbm, own_hess, local_sem.at[2]),
        pltpu.make_async_copy(feat_hbm, feat_in, local_sem.at[3]),
        pltpu.make_async_copy(thr_hbm, thr_in, local_sem.at[4]),
        pltpu.make_async_copy(reg_hbm, reg_in, local_sem.at[5]),
    ]
    barrier = pltpu.get_barrier_semaphore()
    own.start()
    for peer in FEAT_ORDER:
        @pl.when(peer != f)
        def _():
            pl.semaphore_signal(barrier, inc=1, device_id={'feat': peer}, device_id_type=MESH)
    for peer in data_peers:
        pl.semaphore_signal(barrier, inc=1, device_id={'data': peer}, device_id_type=MESH)
    for copy in local:
        copy.start()
    pl.semaphore_wait(barrier, NF - 1 + ND - 1)

    for peer in FEAT_ORDER:
        copy = pltpu.make_async_remote_copy(
            src_ref=bin_hbm, dst_ref=values.at[f], send_sem=feat_send, recv_sem=feat_recv,
            device_id={'feat': peer}, device_id_type=MESH)
        pl.when(peer != f)(copy.start)
    for copy in local:
        copy.wait()
    for peer in range(ND):
        parcels[peer, 0] = own_bins[peer:peer + 1, :].astype(jnp.float32)
        parcels[peer, 1] = own_grad[...]
        parcels[peer, 2] = own_hess[...]
    for peer in data_peers:
        pltpu.make_async_remote_copy(
            src_ref=parcels.at[peer], dst_ref=rows.at[d], send_sem=data_send, recv_sem=data_recv,
            device_id={'data': peer}, device_id_type=MESH).start()
    rows[d] = parcels[d]

    reg_row[...] = jnp.broadcast_to(reg_in[0], (1, 128))
    feat_tbl[...] = jnp.zeros_like(feat_tbl)
    thr_tbl[...] = jnp.zeros_like(thr_tbl)
    feat_tbl[0:7, 0:64] = feat_in[...]
    thr_tbl[0:7, 0:64] = thr_in[...]
    select, threshold = node_tables(feat_tbl[...], thr_tbl[...])
    pltpu.make_async_copy(values, values, feat_recv).wait()
    table = values[...].reshape(NF * 8, CHUNK).astype(jnp.float32).astype(jnp.bfloat16)
    leaves[d] = route(table, select, threshold)

    def leaf_copy(k):
        return pltpu.make_async_remote_copy(
            src_ref=leaves.at[d], dst_ref=leaves.at[d], send_sem=leaf_send, recv_sem=leaf_recv.at[d],
            device_id={'data': data_peers[k]}, device_id_type=MESH)
    for k in range(ND - 1):
        leaf_copy(k).start()

    zero = jnp.float32(0)
    arrived = rows.at[pl.ds(0, ND - 1)]
    pltpu.make_async_copy(arrived, arrived, data_recv).wait()
    sources = [d] + data_peers
    for k, s in enumerate(sources):
        below[k] = jnp.where(rows[s, 0].astype(jnp.int32) <= iota((NBINS, CHUNK), 0), jnp.float32(1), zero).astype(jnp.bfloat16)

    totals = [None, None]
    for k, s in enumerate(sources):
        if k:
            pltpu.make_async_copy(leaves.at[s], leaves.at[s], leaf_recv.at[s]).wait()
        member = leaves[s] == iota((LEAVES, CHUNK), 0)
        mark = jnp.where(member, jnp.float32(1), zero).astype(jnp.bfloat16)
        for part in range(2):
            value = rows[s, 1 + part]
            inside = jnp.where(member, value, zero)
            leaf_sums[s, part] = inside[:, :128] + inside[:, 128:256] + (inside[:, 256:384] + inside[:, 384:])
            product = contract_lanes(jnp.concatenate([mark * piece for piece in split3(value)], axis=0), below[k])
            product = product[:LEAVES] + product[LEAVES:2 * LEAVES] + product[2 * LEAVES:]
            totals[part] = product if k == 0 else totals[part] + product
    for part in range(2):
        for half in range(2):
            sums[part, half] = totals[part][:, 128 * half:128 * (half + 1)]
    sent = values.at[pl.ds(0, NF - 1)]
    pltpu.make_async_copy(sent, sent, feat_send).wait()
    pltpu.make_async_copy(arrived, arrived, data_send).wait()
    told = leaves.at[pl.ds(0, ND - 1)]
    pltpu.make_async_copy(told, told, leaf_send).wait()


def gain_kernel(reg_row, sums, leaf_sums, gain_hbm, leaf_hbm, heap, gains, leaf_row, out_sem):
    reg = reg_row[...]

    def score(g, h):
        return g * g / (h + reg)

    def fill(source, first, start, count):
        for r in range(start, start + count, 8):
            n = min(8, start + count - r)
            rows = pl.ds(r - first, n)
            all_g = source[0, 1, rows, 127:128]
            all_h = source[1, 1, rows, 127:128]
            whole = score(all_g, all_h)
            for half in range(2):
                left_g, left_h = source[0, half, rows, :], source[1, half, rows, :]
                gain = 0.5 * (score(left_g, left_h) + score(all_g - left_g, all_h - left_h) - whole)
                wide = 128 - half
                gains[pl.ds(r, n), 0, pl.ds(128 * half, wide)] = gain[:, :wide]
        send(gains.at[pl.ds(start, count)], gain_hbm.at[pl.ds(start, count)])

    copies = []

    def send(source, target):
        copy = pltpu.make_async_copy(source, target, out_sem.at[len(copies)])
        copy.start()
        copies.append(copy)

    leaf_total = []
    for part in range(2):
        whole = leaf_sums[0, part]
        for s in range(1, ND):
            whole = whole + leaf_sums[s, part]
        leaf_total.append(jnp.sum(whole.T, axis=0, keepdims=True))
    leaf_row[...] = -leaf_total[0] / (leaf_total[1] + reg)
    send(leaf_row, leaf_hbm)
    fill(sums, 127, 127, 64)
    fill(sums, 127, 191, 64)
    for level in range(6, -1, -1):
        n = 2 ** level
        source, base = (sums, 0) if level == 6 else (heap, 2 * n)
        for part in range(2):
            for half in range(2):
                heap[part, half, n:2 * n, :] = (source[part, half, pl.ds(base, n, stride=2), :]
                                                + source[part, half, pl.ds(base + 1, n, stride=2), :])
    fill(heap, -1, 0, 127)
    for copy in copies:
        copy.wait()


def solution(mesh):
    def per_device(binned, gradient, hessian, split_feat, split_thr, reg_lambda):
        hbm = pl.BlockSpec(memory_space=pltpu.HBM)
        vmem = pl.BlockSpec(memory_space=pltpu.VMEM)
        dma = pltpu.SemaphoreType.DMA
        inputs = [binned.T, gradient.reshape(1, CHUNK), hessian.reshape(1, CHUNK), split_feat, split_thr]
        sums, leaf_sums, reg_row = pl.pallas_call(
            exchange_kernel,
            out_shape=[
                jax.ShapeDtypeStruct((2, 2, LEAVES, 128), jnp.float32),
                jax.ShapeDtypeStruct((ND, 2, LEAVES, 128), jnp.float32),
                jax.ShapeDtypeStruct((1, 128), jnp.float32),
            ],
            in_specs=[hbm] * 5 + [pl.BlockSpec(memory_space=pl.ANY)],
            out_specs=[vmem] * 3,
            scratch_shapes=[
                pltpu.VMEM((NF, 8, CHUNK), jnp.int32),
                pltpu.VMEM((ND, 3, 1, CHUNK), jnp.float32),
                pltpu.VMEM((ND, 3, 1, CHUNK), jnp.float32),
                pltpu.VMEM((ND, 1, CHUNK), jnp.int32),
                pltpu.VMEM((ND, NBINS, CHUNK), jnp.bfloat16),
                pltpu.VMEM((8, CHUNK), jnp.int32),
                pltpu.VMEM((1, CHUNK), jnp.float32),
                pltpu.VMEM((1, CHUNK), jnp.float32),
                pltpu.SMEM((1,), jnp.float32),
                pltpu.VMEM((7, 64), jnp.int32),
                pltpu.VMEM((7, 64), jnp.int32),
                pltpu.VMEM((8, 128), jnp.int32),
                pltpu.VMEM((8, 128), jnp.int32),
                dma((6,)), dma, dma, dma, dma, dma, dma((ND,)),
            ],
            compiler_params=pltpu.CompilerParams(collective_id=0, has_side_effects=True, vmem_limit_bytes=24 * 2 ** 20),
            name='exchange',
        )(*[pltpu.with_memory_space_constraint(a, pltpu.HBM) for a in inputs], reg_lambda)
        gain, leaf_value = pl.pallas_call(
            gain_kernel,
            out_shape=[
                jax.ShapeDtypeStruct((255, 1, 255), jnp.float32),
                jax.ShapeDtypeStruct((1, LEAVES), jnp.float32),
            ],
            in_specs=[vmem] * 3,
            out_specs=[hbm] * 2,
            scratch_shapes=[
                pltpu.VMEM((2, 2, LEAVES, 128), jnp.float32),
                pltpu.VMEM((255, 1, 255), jnp.float32),
                pltpu.VMEM((1, LEAVES), jnp.float32),
                dma((4,)),
            ],
            compiler_params=pltpu.CompilerParams(vmem_limit_bytes=24 * 2 ** 20),
            name='gains',
        )(reg_row, sums, leaf_sums)
        return gain, leaf_value.reshape(LEAVES)

    row_spec = P(('tree', 'data'))
    return jax.shard_map(
        per_device,
        mesh=mesh,
        in_specs=(P(('tree', 'data'), 'feat'), row_spec, row_spec, P('tree', None), P('tree', None), P(None)),
        out_specs=(P('tree', ('feat', 'data'), None), P('tree')),
        check_vma=False,
    )
```

time: 24.3 us -> 20.2 us (0.83)
  Pallas kernels: 22.8 us -> 18.8 us
    pallas_call x1, Pallas kernels: 3.85 us -> 1.1 us  [per_device(): pl.pallas_call(gain_kernel, out_shape=[jax.ShapeDtypeStruct((255, 1, 255)...]
    pallas_call x1, Pallas kernels: 19 us -> 17.7 us  [per_device(): pl.pallas_call(exchange_kernel, out_shape=[jax.ShapeDtypeStruct((2, 2, LE...]
where the time goes in v2:
time: 20.2 us; the launch traced here: 20.1 us
  Pallas kernels  18.8 us (93%)
  between operations  1.29 us (6%)
    pallas_call x1, Pallas kernels, per_device(): pl.pallas_call(exchange_kernel, out_shape=[jax.ShapeDtypeStruct((2, 2, LE...  17.7 us
    pallas_call x1, Pallas kernels, per_device(): pl.pallas_call(gain_kernel, out_shape=[jax.ShapeDtypeStruct((255, 1, 255)...  1.1 us

profile of v2, /device:TPU:1, one launch (start us, length us, event | category | flops | bytes accessed | tf_op | source)
XLA Modules:
  0.0 20.1 jit_solution(2531891186748689131)
XLA Ops:
  1.3 17.7 %exchange.1 = (f32[2,2,128,128]{3,2,1,0:T(8,128)S(1)}, f32[8,2,128,128]{3,2,1,0:T(8,128)S(1)}, f32[1,128]{1,0:T(1,128)S(1)}) custom-call(s32[8,512]{1,0:T(8,128)} %bitcast.4, f32[1,512]{1,0:T(1,128)} %bitcast.5, f32[1,512]{1,0:T(1,128)} %bitcast.6, s32[7,64]{1,0:T(8,128)} %feat_hbm.1, s32[7,64]{1,0:T(8,128)} %thr_hbm.1, f32[1]{0:T(128)S(6)} %copy.8.reg_hbm), custom_call_target="tpu_custom_call" | custom-call | tf_op jit(solution)/shard_map/exchange/pallas_call | solution.py:216
  19.0 1.1 %gains.1 = (f32[255,1,255]{2,1,0:T(1,128)}, f32[1,128]{1,0:T(1,128)}) custom-call(f32[1,128]{1,0:T(1,128)S(1)} %get-tuple-element.7.reg_row, f32[2,2,128,128]{3,2,1,0:T(8,128)S(1)} %get-tuple-element.8.sums, f32[8,2,128,128]{3,2,1,0:T(8,128)S(1)} %get-tuple-element.9.leaf_sums), custom_call_target="tpu_custom_call" | custom-call | tf_op jit(solution)/shard_map/gains/pallas_call | solution.py:244

commit v3 on v2

--- a/solution.py
+++ b/solution.py
@@ -11,7 +11,10 @@
 ND = 8
 CHUNK = 512
 LEAVES = 128
-FEAT_ORDER = sorted(range(NF), key=lambda f: min(f // SIDE, SIDE - f // SIDE) + min(f % SIDE, SIDE - f % SIDE))
+HUB = 1
+FEAT_ORDER = (0, 1, 4, 2, 5, 3, 8, 6, 9, 7, 10, 11, 12, 13, 14, 15)
+FEAT_RANK = [FEAT_ORDER.index(f) for f in range(NF)]
+DATA_ORDER = (1, 0, 3, 2, 5, 4, 7, 6)
 MESH = pl.DeviceIdType.MESH
 
 
@@ -66,14 +69,18 @@
 
 def exchange_kernel(bin_hbm, grad_hbm, hess_hbm, feat_hbm, thr_hbm, reg_hbm, sums, leaf_sums, reg_row,
                     values, parcels, rows, leaves, below, own_bins, own_grad, own_hess, reg_in, feat_in, thr_in, feat_tbl, thr_tbl,
-                    local_sem, feat_send, feat_recv, data_send, data_recv, leaf_send, leaf_recv):
+                    local_sem, ready, gathered, everyone, earlier_ok, later_ok,
+                    block_send, block_recv, data_send, data_recv, leaf_send, leaf_recv):
     f, d = lax.axis_index('feat'), lax.axis_index('data')
     x, core = d // 2, d % 2
+    chief, other = 2 * x + 1, 2 * x + 1 - core
     near = x + 1 - 2 * (x % 2)
-    lines = [near, SIDE - 1 - x, (x + 2) % SIDE]
-    data_peers = [2 * x + 1 - core] + [2 * line + c for c in (1, 0) for line in lines]
-
-    own = pltpu.make_async_copy(bin_hbm, values.at[f], feat_recv)
+    lines = [near, (x + 2) % SIDE, SIDE - 1 - x]
+    data_peers = [other] + [2 * line + c for c in (1, 0) for line in lines]
+    rank = sum(jnp.where(f == peer, FEAT_RANK[peer], 0) for peer in range(NF))
+    is_chief = core == 1
+
+    own = pltpu.make_async_copy(bin_hbm, values.at[1, f], block_recv.at[1])
     local = [
         pltpu.make_async_copy(bin_hbm, own_bins, local_sem.at[0]),
         pltpu.make_async_copy(grad_hbm, own_grad, local_sem.at[1]),
@@ -83,62 +90,118 @@
         pltpu.make_async_copy(reg_hbm, reg_in, local_sem.at[5]),
     ]
     barrier = pltpu.get_barrier_semaphore()
-    own.start()
-    for peer in FEAT_ORDER:
-        @pl.when(peer != f)
+
+    def signal(semaphore, **device):
+        pl.semaphore_signal(semaphore, inc=1, device_id=device, device_id_type=MESH)
+
+    def send_block(peer, group):
+        pltpu.make_async_remote_copy(
+            src_ref=bin_hbm, dst_ref=values.at[group, f], send_sem=block_send, recv_sem=block_recv.at[group],
+            device_id={'feat': peer, 'data': chief}, device_id_type=MESH).start()
+
+    @pl.when(is_chief)
+    def _():
+        for peer in reversed(FEAT_ORDER):
+            pl.when(FEAT_RANK[peer] > rank)(lambda: signal(barrier, feat=peer))
+        signal(barrier, data=other)
+
+        @pl.when(d == HUB)
         def _():
-            pl.semaphore_signal(barrier, inc=1, device_id={'feat': peer}, device_id_type=MESH)
-    for peer in data_peers:
-        pl.semaphore_signal(barrier, inc=1, device_id={'data': peer}, device_id_type=MESH)
+            for peer in data_peers:
+                signal(barrier, data=peer)
+        own.start()
+    pl.when(jnp.logical_not(is_chief))(lambda: signal(barrier, data=other))
     for copy in local:
         copy.start()
-    pl.semaphore_wait(barrier, NF - 1 + ND - 1)
-
-    for peer in FEAT_ORDER:
-        copy = pltpu.make_async_remote_copy(
-            src_ref=bin_hbm, dst_ref=values.at[f], send_sem=feat_send, recv_sem=feat_recv,
-            device_id={'feat': peer}, device_id_type=MESH)
-        pl.when(peer != f)(copy.start)
+
+    @pl.when(is_chief)
+    def _():
+        pl.semaphore_wait(barrier, rank + 1 + jnp.where(d == HUB, 0, 1))
+        signal(earlier_ok, data=other)
+        for peer in FEAT_ORDER:
+            pl.when(FEAT_RANK[peer] < rank)(lambda: send_block(peer, 1))
+        for peer in FEAT_ORDER:
+            pl.when(FEAT_RANK[peer] < rank)(lambda: signal(ready, feat=peer))
+        pl.when(d != HUB)(lambda: signal(gathered, data=HUB))
+
+    @pl.when(jnp.logical_not(is_chief))
+    def _():
+        pl.semaphore_wait(barrier, 2)
+        signal(gathered, data=HUB)
+        pl.semaphore_wait(earlier_ok, 1)
+        for peer in FEAT_ORDER:
+            pl.when(FEAT_RANK[peer] <= rank)(lambda: send_block(peer, 0))
+
     for copy in local:
         copy.wait()
     for peer in range(ND):
         parcels[peer, 0] = own_bins[peer:peer + 1, :].astype(jnp.float32)
         parcels[peer, 1] = own_grad[...]
         parcels[peer, 2] = own_hess[...]
+    rows[d] = parcels[d]
+
+    @pl.when(d == HUB)
+    def _():
+        pl.semaphore_wait(gathered, ND - 1)
+        for peer in data_peers:
+            signal(everyone, data=peer)
+
+    @pl.when(d != HUB)
+    def _():
+        pl.semaphore_wait(everyone, 1)
     for peer in data_peers:
         pltpu.make_async_remote_copy(
             src_ref=parcels.at[peer], dst_ref=rows.at[d], send_sem=data_send, recv_sem=data_recv,
             device_id={'data': peer}, device_id_type=MESH).start()
-    rows[d] = parcels[d]
+
+    @pl.when(is_chief)
+    def _():
+        pl.when(rank < NF - 1)(lambda: pl.semaphore_wait(ready, NF - 1 - rank))
+        signal(later_ok, data=other)
+        for peer in FEAT_ORDER:
+            pl.when(FEAT_RANK[peer] > rank)(lambda: send_block(peer, 1))
+
+    @pl.when(jnp.logical_not(is_chief))
+    def _():
+        pl.semaphore_wait(later_ok, 1)
+        for peer in FEAT_ORDER:
+            pl.when(FEAT_RANK[peer] > rank)(lambda: send_block(peer, 0))
 
     reg_row[...] = jnp.broadcast_to(reg_in[0], (1, 128))
-    feat_tbl[...] = jnp.zeros_like(feat_tbl)
-    thr_tbl[...] = jnp.zeros_like(thr_tbl)
-    feat_tbl[0:7, 0:64] = feat_in[...]
-    thr_tbl[0:7, 0:64] = thr_in[...]
-    select, threshold = node_tables(feat_tbl[...], thr_tbl[...])
-    pltpu.make_async_copy(values, values, feat_recv).wait()
-    table = values[...].reshape(NF * 8, CHUNK).astype(jnp.float32).astype(jnp.bfloat16)
-    leaves[d] = route(table, select, threshold)
-
-    def leaf_copy(k):
-        return pltpu.make_async_remote_copy(
-            src_ref=leaves.at[d], dst_ref=leaves.at[d], send_sem=leaf_send, recv_sem=leaf_recv.at[d],
-            device_id={'data': data_peers[k]}, device_id_type=MESH)
-    for k in range(ND - 1):
-        leaf_copy(k).start()
-
     zero = jnp.float32(0)
     arrived = rows.at[pl.ds(0, ND - 1)]
     pltpu.make_async_copy(arrived, arrived, data_recv).wait()
-    sources = [d] + data_peers
+    sources = [chief, chief - 1] + data_peers[1:]
     for k, s in enumerate(sources):
         below[k] = jnp.where(rows[s, 0].astype(jnp.int32) <= iota((NBINS, CHUNK), 0), jnp.float32(1), zero).astype(jnp.bfloat16)
 
+    @pl.when(is_chief)
+    def _():
+        feat_tbl[...] = jnp.zeros_like(feat_tbl)
+        thr_tbl[...] = jnp.zeros_like(thr_tbl)
+        feat_tbl[0:7, 0:64] = feat_in[...]
+        thr_tbl[0:7, 0:64] = thr_in[...]
+        select, threshold = node_tables(feat_tbl[...], thr_tbl[...])
+        for group in (1, 0):
+            block = values.at[group]
+            pltpu.make_async_copy(block, block, block_recv.at[group]).wait()
+            s = chief - 1 + group
+            table = values[group].reshape(NF * 8, CHUNK).astype(jnp.float32).astype(jnp.bfloat16)
+            leaves[s] = route(table, select, threshold)
+            for peer in DATA_ORDER:
+                @pl.when(peer != d)
+                def _():
+                    pltpu.make_async_remote_copy(
+                        src_ref=leaves.at[s], dst_ref=leaves.at[s], send_sem=leaf_send, recv_sem=leaf_recv.at[s],
+                        device_id={'data': peer}, device_id_type=MESH).start()
+
     totals = [None, None]
     for k, s in enumerate(sources):
-        if k:
-            pltpu.make_async_copy(leaves.at[s], leaves.at[s], leaf_recv.at[s]).wait()
+        arrival = pltpu.make_async_copy(leaves.at[s], leaves.at[s], leaf_recv.at[s])
+        if k < 2:
+            pl.when(jnp.logical_not(is_chief))(arrival.wait)
+        else:
+            arrival.wait()
         member = leaves[s] == iota((LEAVES, CHUNK), 0)
         mark = jnp.where(member, jnp.float32(1), zero).astype(jnp.bfloat16)
         for part in range(2):
@@ -151,11 +214,20 @@
     for part in range(2):
         for half in range(2):
             sums[part, half] = totals[part][:, 128 * half:128 * (half + 1)]
-    sent = values.at[pl.ds(0, NF - 1)]
-    pltpu.make_async_copy(sent, sent, feat_send).wait()
+
+    @pl.when(is_chief)
+    def _():
+        sent = values.at[0, pl.ds(0, NF - 1)]
+        pltpu.make_async_copy(sent, sent, block_send).wait()
+        told = leaves.at[pl.ds(0, ND - 1)]
+        pltpu.make_async_copy(told, told, leaf_send).wait()
+        pltpu.make_async_copy(told, told, leaf_send).wait()
+
+    @pl.when(jnp.logical_not(is_chief))
+    def _():
+        sent = values.at[0]
+        pltpu.make_async_copy(sent, sent, block_send).wait()
     pltpu.make_async_copy(arrived, arrived, data_send).wait()
-    told = leaves.at[pl.ds(0, ND - 1)]
-    pltpu.make_async_copy(told, told, leaf_send).wait()
 
 
 def gain_kernel(reg_row, sums, leaf_sums, gain_hbm, leaf_hbm, heap, gains, leaf_row, out_sem):
@@ -211,7 +283,7 @@
     def per_device(binned, gradient, hessian, split_feat, split_thr, reg_lambda):
         hbm = pl.BlockSpec(memory_space=pltpu.HBM)
         vmem = pl.BlockSpec(memory_space=pltpu.VMEM)
-        dma = pltpu.SemaphoreType.DMA
+        dma, regular = pltpu.SemaphoreType.DMA, pltpu.SemaphoreType.REGULAR
         inputs = [binned.T, gradient.reshape(1, CHUNK), hessian.reshape(1, CHUNK), split_feat, split_thr]
         sums, leaf_sums, reg_row = pl.pallas_call(
             exchange_kernel,
@@ -223,7 +295,7 @@
             in_specs=[hbm] * 5 + [pl.BlockSpec(memory_space=pl.ANY)],
             out_specs=[vmem] * 3,
             scratch_shapes=[
-                pltpu.VMEM((NF, 8, CHUNK), jnp.int32),
+                pltpu.VMEM((2, NF, 8, CHUNK), jnp.int32),
                 pltpu.VMEM((ND, 3, 1, CHUNK), jnp.float32),
                 pltpu.VMEM((ND, 3, 1, CHUNK), jnp.float32),
                 pltpu.VMEM((ND, 1, CHUNK), jnp.int32),
@@ -236,7 +308,8 @@
                 pltpu.VMEM((7, 64), jnp.int32),
                 pltpu.VMEM((8, 128), jnp.int32),
                 pltpu.VMEM((8, 128), jnp.int32),
-                dma((6,)), dma, dma, dma, dma, dma, dma((ND,)),
+                dma((6,)), regular, regular, regular, regular, regular,
+                dma, dma((2,)), dma, dma, dma, dma((ND,)),
             ],
             compiler_params=pltpu.CompilerParams(collective_id=0, has_side_effects=True, vmem_limit_bytes=24 * 2 ** 20),
             name='exchange',

time: 20.2 us -> 18.4 us (0.911); the launches traced: 20.1 us -> 18.1 us
  Pallas kernels: 18.8 us -> 16.8 us
    pallas_call x1, Pallas kernels: 17.7 us -> 15.7 us  [per_device(): pl.pallas_call(exchange_kernel, out_shape=[jax.ShapeDtypeStruct((2, 2, LE...]
where the time goes in v3:
time: 18.4 us; the launch traced here: 18.1 us
  Pallas kernels  16.8 us (91%)
  between operations  1.29 us (7%)
    pallas_call x1, Pallas kernels, per_device(): pl.pallas_call(exchange_kernel, out_shape=[jax.ShapeDtypeStruct((2, 2, LE...  15.7 us
    pallas_call x1, Pallas kernels, per_device(): pl.pallas_call(gain_kernel, out_shape=[jax.ShapeDtypeStruct((255, 1, 255)...  1.1 us

profile of v3, /device:TPU:1, one launch (start us, length us, event | category | flops | bytes accessed | tf_op | source)
XLA Modules:
  0.0 18.1 jit_solution(3226309544189437027)
XLA Ops:
  1.3 15.7 %exchange.1 = (f32[2,2,128,128]{3,2,1,0:T(8,128)S(1)}, f32[8,2,128,128]{3,2,1,0:T(8,128)S(1)}, f32[1,128]{1,0:T(1,128)S(1)}) custom-call(s32[8,512]{1,0:T(8,128)} %bitcast.4, f32[1,512]{1,0:T(1,128)} %bitcast.5, f32[1,512]{1,0:T(1,128)} %bitcast.6, s32[7,64]{1,0:T(8,128)} %feat_hbm.1, s32[7,64]{1,0:T(8,128)} %thr_hbm.1, f32[1]{0:T(128)S(6)} %copy.8.reg_hbm), custom_call_target="tpu_custom_call" | custom-call | tf_op jit(solution)/shard_map/exchange/pallas_call | solution.py:288
  17.0 1.1 %gains.1 = (f32[255,1,255]{2,1,0:T(1,128)}, f32[1,128]{1,0:T(1,128)}) custom-call(f32[1,128]{1,0:T(1,128)S(1)} %get-tuple-element.7.reg_row, f32[2,2,128,128]{3,2,1,0:T(8,128)S(1)} %get-tuple-element.8.sums, f32[8,2,128,128]{3,2,1,0:T(8,128)S(1)} %get-tuple-element.9.leaf_sums), custom_call_target="tpu_custom_call" | custom-call | tf_op jit(solution)/shard_map/gains/pallas_call | solution.py:317

commit v4 on v3

--- a/solution.py
+++ b/solution.py
@@ -11,9 +11,10 @@
 ND = 8
 CHUNK = 512
 LEAVES = 128
-HUB = 1
-FEAT_ORDER = (0, 1, 4, 2, 5, 3, 8, 6, 9, 7, 10, 11, 12, 13, 14, 15)
+HUB = 0
+FEAT_ORDER = (0, 1, 4, 2, 3, 5, 8, 10, 7, 9, 12, 6, 11, 14, 15, 13)
 FEAT_RANK = [FEAT_ORDER.index(f) for f in range(NF)]
+BUILD = {0: (0,), 1: (1,), 2: (2, 3), 3: (4, 5, 6, 7)}
 DATA_ORDER = (1, 0, 3, 2, 5, 4, 7, 6)
 MESH = pl.DeviceIdType.MESH
 
@@ -67,8 +68,8 @@
     return leaf
 
 
-def exchange_kernel(bin_hbm, grad_hbm, hess_hbm, feat_hbm, thr_hbm, reg_hbm, sums, leaf_sums, reg_row,
-                    values, parcels, rows, leaves, below, own_bins, own_grad, own_hess, reg_in, feat_in, thr_in, feat_tbl, thr_tbl,
+def exchange_kernel(bin_hbm, grad_hbm, hess_hbm, feat_hbm, thr_hbm, reg_hbm, sums, leaf_row, reg_row,
+                    leaf_sums, values, parcels, rows, columns, leaves, below, own_bins, own_grad, own_hess, reg_in, feat_in, thr_in, feat_tbl, thr_tbl,
                     local_sem, ready, gathered, everyone, earlier_ok, later_ok,
                     block_send, block_recv, data_send, data_recv, leaf_send, leaf_recv):
     f, d = lax.axis_index('feat'), lax.axis_index('data')
@@ -104,30 +105,32 @@
         for peer in reversed(FEAT_ORDER):
             pl.when(FEAT_RANK[peer] > rank)(lambda: signal(barrier, feat=peer))
         signal(barrier, data=other)
+        own.start()
+
+    @pl.when(jnp.logical_not(is_chief))
+    def _():
+        signal(barrier, data=other)
 
         @pl.when(d == HUB)
         def _():
-            for peer in data_peers:
+            for peer in range(2, ND, 2):
                 signal(barrier, data=peer)
-        own.start()
-    pl.when(jnp.logical_not(is_chief))(lambda: signal(barrier, data=other))
     for copy in local:
         copy.start()
 
     @pl.when(is_chief)
     def _():
-        pl.semaphore_wait(barrier, rank + 1 + jnp.where(d == HUB, 0, 1))
+        pl.semaphore_wait(barrier, rank + 1)
         signal(earlier_ok, data=other)
         for peer in FEAT_ORDER:
             pl.when(FEAT_RANK[peer] < rank)(lambda: send_block(peer, 1))
         for peer in FEAT_ORDER:
             pl.when(FEAT_RANK[peer] < rank)(lambda: signal(ready, feat=peer))
+
+    @pl.when(jnp.logical_not(is_chief))
+    def _():
+        pl.semaphore_wait(barrier, jnp.where(d == HUB, 1, 2))
         pl.when(d != HUB)(lambda: signal(gathered, data=HUB))
-
-    @pl.when(jnp.logical_not(is_chief))
-    def _():
-        pl.semaphore_wait(barrier, 2)
-        signal(gathered, data=HUB)
         pl.semaphore_wait(earlier_ok, 1)
         for peer in FEAT_ORDER:
             pl.when(FEAT_RANK[peer] <= rank)(lambda: send_block(peer, 0))
@@ -142,7 +145,7 @@
 
     @pl.when(d == HUB)
     def _():
-        pl.semaphore_wait(gathered, ND - 1)
+        pl.semaphore_wait(gathered, SIDE - 1)
         for peer in data_peers:
             signal(everyone, data=peer)
 
@@ -169,11 +172,7 @@
 
     reg_row[...] = jnp.broadcast_to(reg_in[0], (1, 128))
     zero = jnp.float32(0)
-    arrived = rows.at[pl.ds(0, ND - 1)]
-    pltpu.make_async_copy(arrived, arrived, data_recv).wait()
     sources = [chief, chief - 1] + data_peers[1:]
-    for k, s in enumerate(sources):
-        below[k] = jnp.where(rows[s, 0].astype(jnp.int32) <= iota((NBINS, CHUNK), 0), jnp.float32(1), zero).astype(jnp.bfloat16)
 
     @pl.when(is_chief)
     def _():
@@ -195,8 +194,17 @@
                         src_ref=leaves.at[s], dst_ref=leaves.at[s], send_sem=leaf_send, recv_sem=leaf_recv.at[s],
                         device_id={'data': peer}, device_id_type=MESH).start()
 
+    arrived = rows.at[pl.ds(0, ND - 1)]
+    pltpu.make_async_copy(arrived, arrived, data_recv).wait()
+    columns[...] = jnp.concatenate([rows[s, 0] for s in sources], axis=0).T
+
+    def build(k):
+        below[k] = jnp.where(columns[:, k:k + 1] <= iota((CHUNK, NBINS), 1).astype(jnp.float32), jnp.float32(1), zero).astype(jnp.bfloat16)
+
     totals = [None, None]
     for k, s in enumerate(sources):
+        for later in BUILD.get(k, ()):
+            build(later)
         arrival = pltpu.make_async_copy(leaves.at[s], leaves.at[s], leaf_recv.at[s])
         if k < 2:
             pl.when(jnp.logical_not(is_chief))(arrival.wait)
@@ -208,9 +216,16 @@
             value = rows[s, 1 + part]
             inside = jnp.where(member, value, zero)
             leaf_sums[s, part] = inside[:, :128] + inside[:, 128:256] + (inside[:, 256:384] + inside[:, 384:])
-            product = contract_lanes(jnp.concatenate([mark * piece for piece in split3(value)], axis=0), below[k])
+            product = jnp.dot(jnp.concatenate([mark * piece for piece in split3(value)], axis=0), below[k], preferred_element_type=jnp.float32)
             product = product[:LEAVES] + product[LEAVES:2 * LEAVES] + product[2 * LEAVES:]
             totals[part] = product if k == 0 else totals[part] + product
+    leaf_total = []
+    for part in range(2):
+        whole = leaf_sums[0, part]
+        for s in range(1, ND):
+            whole = whole + leaf_sums[s, part]
+        leaf_total.append(jnp.sum(whole.T, axis=0, keepdims=True))
+    leaf_row[...] = -leaf_total[0] / (leaf_total[1] + reg_row[...])
     for part in range(2):
         for half in range(2):
             sums[part, half] = totals[part][:, 128 * half:128 * (half + 1)]
@@ -230,7 +245,7 @@
     pltpu.make_async_copy(arrived, arrived, data_send).wait()
 
 
-def gain_kernel(reg_row, sums, leaf_sums, gain_hbm, leaf_hbm, heap, gains, leaf_row, out_sem):
+def gain_kernel(reg_row, sums, leaf_row, gain_hbm, leaf_hbm, heap, gains, out_sem):
     reg = reg_row[...]
 
     def score(g, h):
@@ -257,13 +272,6 @@
         copy.start()
         copies.append(copy)
 
-    leaf_total = []
-    for part in range(2):
-        whole = leaf_sums[0, part]
-        for s in range(1, ND):
-            whole = whole + leaf_sums[s, part]
-        leaf_total.append(jnp.sum(whole.T, axis=0, keepdims=True))
-    leaf_row[...] = -leaf_total[0] / (leaf_total[1] + reg)
     send(leaf_row, leaf_hbm)
     fill(sums, 127, 127, 64)
     fill(sums, 127, 191, 64)
@@ -285,21 +293,23 @@
         vmem = pl.BlockSpec(memory_space=pltpu.VMEM)
         dma, regular = pltpu.SemaphoreType.DMA, pltpu.SemaphoreType.REGULAR
         inputs = [binned.T, gradient.reshape(1, CHUNK), hessian.reshape(1, CHUNK), split_feat, split_thr]
-        sums, leaf_sums, reg_row = pl.pallas_call(
+        sums, leaf_row, reg_row = pl.pallas_call(
             exchange_kernel,
             out_shape=[
                 jax.ShapeDtypeStruct((2, 2, LEAVES, 128), jnp.float32),
-                jax.ShapeDtypeStruct((ND, 2, LEAVES, 128), jnp.float32),
+                jax.ShapeDtypeStruct((1, LEAVES), jnp.float32),
                 jax.ShapeDtypeStruct((1, 128), jnp.float32),
             ],
             in_specs=[hbm] * 5 + [pl.BlockSpec(memory_space=pl.ANY)],
             out_specs=[vmem] * 3,
             scratch_shapes=[
+                pltpu.VMEM((ND, 2, LEAVES, 128), jnp.float32),
                 pltpu.VMEM((2, NF, 8, CHUNK), jnp.int32),
                 pltpu.VMEM((ND, 3, 1, CHUNK), jnp.float32),
                 pltpu.VMEM((ND, 3, 1, CHUNK), jnp.float32),
+                pltpu.VMEM((CHUNK, ND), jnp.float32),
                 pltpu.VMEM((ND, 1, CHUNK), jnp.int32),
-                pltpu.VMEM((ND, NBINS, CHUNK), jnp.bfloat16),
+                pltpu.VMEM((ND, CHUNK, NBINS), jnp.bfloat16),
                 pltpu.VMEM((8, CHUNK), jnp.int32),
                 pltpu.VMEM((1, CHUNK), jnp.float32),
                 pltpu.VMEM((1, CHUNK), jnp.float32),
@@ -325,12 +335,11 @@
             scratch_shapes=[
                 pltpu.VMEM((2, 2, LEAVES, 128), jnp.float32),
                 pltpu.VMEM((255, 1, 255), jnp.float32),
-                pltpu.VMEM((1, LEAVES), jnp.float32),
                 dma((4,)),
             ],
             compiler_params=pltpu.CompilerParams(vmem_limit_bytes=24 * 2 ** 20),
             name='gains',
-        )(reg_row, sums, leaf_sums)
+        )(reg_row, sums, leaf_row)
         return gain, leaf_value.reshape(LEAVES)
 
     row_spec = P(('tree', 'data'))

time: 18.4 us -> 18 us (0.978)
  Pallas kernels: 16.8 us -> 16.5 us
    pallas_call x1, Pallas kernels: 15.7 us -> 15.5 us  [per_device(): pl.pallas_call(exchange_kernel, out_shape=[jax.ShapeDtypeStruct((2, 2, LE...]
where the time goes in v4:
time: 18 us; the launch traced here: 17.8 us
  Pallas kernels  16.5 us (92%)
  between operations  1.29 us (7%)
    pallas_call x1, Pallas kernels, per_device(): pl.pallas_call(exchange_kernel, out_shape=[jax.ShapeDtypeStruct((2, 2, LE...  15.5 us
    pallas_call x1, Pallas kernels, per_device(): pl.pallas_call(gain_kernel, out_shape=[jax.ShapeDtypeStruct((255, 1, 255)...  1.04 us

profile of v4, /device:TPU:1, one launch (start us, length us, event | category | flops | bytes accessed | tf_op | source)
XLA Modules:
  0.0 17.8 jit_solution(1420358125237723651)
XLA Ops:
  1.3 15.5 %exchange.1 = (f32[2,2,128,128]{3,2,1,0:T(8,128)S(1)}, f32[1,128]{1,0:T(1,128)S(1)}, f32[1,128]{1,0:T(1,128)S(1)}) custom-call(s32[8,512]{1,0:T(8,128)} %bitcast.4, f32[1,512]{1,0:T(1,128)} %bitcast.5, f32[1,512]{1,0:T(1,128)} %bitcast.6, s32[7,64]{1,0:T(8,128)} %feat_hbm.1, s32[7,64]{1,0:T(8,128)} %thr_hbm.1, f32[1]{0:T(128)S(6)} %copy.8.reg_hbm), custom_call_target="tpu_custom_call" | custom-call | tf_op jit(solution)/shard_map/exchange/pallas_call | solution.py:296
  16.8 1.0 %gains.1 = (f32[255,1,255]{2,1,0:T(1,128)}, f32[1,128]{1,0:T(1,128)}) custom-call(f32[1,128]{1,0:T(1,128)S(1)} %get-tuple-element.7.reg_row, f32[2,2,128,128]{3,2,1,0:T(8,128)S(1)} %get-tuple-element.8.sums, f32[1,128]{1,0:T(1,128)S(1)} %get-tuple-element.9.leaf_row), custom_call_target="tpu_custom_call" | custom-call | tf_op jit(solution)/shard_map/gains/pallas_call | solution.py:327

commit v5 on v4

--- a/solution.py
+++ b/solution.py
@@ -12,9 +12,11 @@
 CHUNK = 512
 LEAVES = 128
 HUB = 0
-FEAT_ORDER = (0, 1, 4, 2, 3, 5, 8, 10, 7, 9, 12, 6, 11, 14, 15, 13)
+FEAT_ORDER = (0, 1, 2, 4, 3, 8, 9, 7, 5, 12, 6, 10, 11, 14, 13, 15)
 FEAT_RANK = [FEAT_ORDER.index(f) for f in range(NF)]
 BUILD = {0: (0,), 1: (1,), 2: (2, 3), 3: (4, 5, 6, 7)}
+SEND_ORDER = (0, 8, 15, 3, 2, 13, 4, 1, 5, 14, 7, 9, 11, 6, 12, 10)
+RANK_GROUPS = ((0, 7), (8, 15))
 DATA_ORDER = (1, 0, 3, 2, 5, 4, 7, 6)
 MESH = pl.DeviceIdType.MESH
 
@@ -122,17 +124,18 @@
     def _():
         pl.semaphore_wait(barrier, rank + 1)
         signal(earlier_ok, data=other)
+        for peer in SEND_ORDER:
+            pl.when(FEAT_RANK[peer] < rank)(lambda: send_block(peer, 1))
+        own_group = sum(jnp.where(rank >= first, 1, 0) for first, _ in RANK_GROUPS) - 1
         for peer in FEAT_ORDER:
-            pl.when(FEAT_RANK[peer] < rank)(lambda: send_block(peer, 1))
-        for peer in FEAT_ORDER:
-            pl.when(FEAT_RANK[peer] < rank)(lambda: signal(ready, feat=peer))
+            pl.when(FEAT_RANK[peer] < rank)(lambda: signal(ready.at[own_group], feat=peer))
 
     @pl.when(jnp.logical_not(is_chief))
     def _():
         pl.semaphore_wait(barrier, jnp.where(d == HUB, 1, 2))
         pl.when(d != HUB)(lambda: signal(gathered, data=HUB))
         pl.semaphore_wait(earlier_ok, 1)
-        for peer in FEAT_ORDER:
+        for peer in SEND_ORDER:
             pl.when(FEAT_RANK[peer] <= rank)(lambda: send_block(peer, 0))
 
     for copy in local:
@@ -157,18 +160,21 @@
             src_ref=parcels.at[peer], dst_ref=rows.at[d], send_sem=data_send, recv_sem=data_recv,
             device_id={'data': peer}, device_id_type=MESH).start()
 
-    @pl.when(is_chief)
-    def _():
-        pl.when(rank < NF - 1)(lambda: pl.semaphore_wait(ready, NF - 1 - rank))
-        signal(later_ok, data=other)
-        for peer in FEAT_ORDER:
-            pl.when(FEAT_RANK[peer] > rank)(lambda: send_block(peer, 1))
-
-    @pl.when(jnp.logical_not(is_chief))
-    def _():
-        pl.semaphore_wait(later_ok, 1)
-        for peer in FEAT_ORDER:
-            pl.when(FEAT_RANK[peer] > rank)(lambda: send_block(peer, 0))
+    for group, (first, last) in enumerate(RANK_GROUPS):
+        count = last - jnp.maximum(rank, first - 1)
+
+        @pl.when(is_chief & (count > 0))
+        def _():
+            pl.semaphore_wait(ready.at[group], count)
+            signal(later_ok, data=other)
+            for peer in FEAT_ORDER[first:last + 1]:
+                pl.when(FEAT_RANK[peer] > rank)(lambda: send_block(peer, 1))
+
+        @pl.when(jnp.logical_not(is_chief) & (count > 0))
+        def _():
+            pl.semaphore_wait(later_ok, 1)
+            for peer in FEAT_ORDER[first:last + 1]:
+                pl.when(FEAT_RANK[peer] > rank)(lambda: send_block(peer, 0))
 
     reg_row[...] = jnp.broadcast_to(reg_in[0], (1, 128))
     zero = jnp.float32(0)
@@ -263,18 +269,10 @@
                 gain = 0.5 * (score(left_g, left_h) + score(all_g - left_g, all_h - left_h) - whole)
                 wide = 128 - half
                 gains[pl.ds(r, n), 0, pl.ds(128 * half, wide)] = gain[:, :wide]
-        send(gains.at[pl.ds(start, count)], gain_hbm.at[pl.ds(start, count)])
-
-    copies = []
-
-    def send(source, target):
-        copy = pltpu.make_async_copy(source, target, out_sem.at[len(copies)])
-        copy.start()
-        copies.append(copy)
-
-    send(leaf_row, leaf_hbm)
-    fill(sums, 127, 127, 64)
-    fill(sums, 127, 191, 64)
+        pltpu.make_async_copy(gains.at[pl.ds(start, count)], gain_hbm.at[pl.ds(start, count)], out_sem.at[0]).start()
+
+    leaf_copy = pltpu.make_async_copy(leaf_row, leaf_hbm, out_sem.at[1])
+    leaf_copy.start()
     for level in range(6, -1, -1):
         n = 2 ** level
         source, base = (sums, 0) if level == 6 else (heap, 2 * n)
@@ -283,8 +281,10 @@
                 heap[part, half, n:2 * n, :] = (source[part, half, pl.ds(base, n, stride=2), :]
                                                 + source[part, half, pl.ds(base + 1, n, stride=2), :])
     fill(heap, -1, 0, 127)
-    for copy in copies:
-        copy.wait()
+    fill(sums, 127, 127, 64)
+    fill(sums, 127, 191, 64)
+    leaf_copy.wait()
+    pltpu.make_async_copy(gains, gain_hbm, out_sem.at[0]).wait()
 
 
 def solution(mesh):
@@ -318,7 +318,7 @@
                 pltpu.VMEM((7, 64), jnp.int32),
                 pltpu.VMEM((8, 128), jnp.int32),
                 pltpu.VMEM((8, 128), jnp.int32),
-                dma((6,)), regular, regular, regular, regular, regular,
+                dma((6,)), regular((len(RANK_GROUPS),)), regular, regular, regular, regular,
                 dma, dma((2,)), dma, dma, dma, dma((ND,)),
             ],
             compiler_params=pltpu.CompilerParams(collective_id=0, has_side_effects=True, vmem_limit_bytes=24 * 2 ** 20),
@@ -335,7 +335,7 @@
             scratch_shapes=[
                 pltpu.VMEM((2, 2, LEAVES, 128), jnp.float32),
                 pltpu.VMEM((255, 1, 255), jnp.float32),
-                dma((4,)),
+                dma((2,)),
             ],
             compiler_params=pltpu.CompilerParams(vmem_limit_bytes=24 * 2 ** 20),
             name='gains',

time: 18 us -> 17.6 us (0.978)
  Pallas kernels: 16.5 us -> 16.1 us
    pallas_call x1, Pallas kernels: 15.5 us -> 15.1 us  [per_device(): pl.pallas_call(exchange_kernel, out_shape=[jax.ShapeDtypeStruct((2, 2, LE...]
where the time goes in v5:
time: 17.6 us; the launch traced here: 17.4 us
  Pallas kernels  16.1 us (91%)
  between operations  1.29 us (7%)
    pallas_call x1, Pallas kernels, per_device(): pl.pallas_call(exchange_kernel, out_shape=[jax.ShapeDtypeStruct((2, 2, LE...  15.1 us
    pallas_call x1, Pallas kernels, per_device(): pl.pallas_call(gain_kernel, out_shape=[jax.ShapeDtypeStruct((255, 1, 255)...  0.99 us

profile of v5, /device:TPU:1, one launch (start us, length us, event | category | flops | bytes accessed | tf_op | source)
XLA Modules:
  0.0 17.4 jit_solution(10361111710690336998)
XLA Ops:
  1.3 15.1 %exchange.1 = (f32[2,2,128,128]{3,2,1,0:T(8,128)S(1)}, f32[1,128]{1,0:T(1,128)S(1)}, f32[1,128]{1,0:T(1,128)S(1)}) custom-call(s32[8,512]{1,0:T(8,128)} %bitcast.4, f32[1,512]{1,0:T(1,128)} %bitcast.5, f32[1,512]{1,0:T(1,128)} %bitcast.6, s32[7,64]{1,0:T(8,128)} %feat_hbm.1, s32[7,64]{1,0:T(8,128)} %thr_hbm.1, f32[1]{0:T(128)S(6)} %copy.8.reg_hbm), custom_call_target="tpu_custom_call" | custom-call | tf_op jit(solution)/shard_map/exchange/pallas_call | solution.py:296
  16.4 1.0 %gains.1 = (f32[255,1,255]{2,1,0:T(1,128)}, f32[1,128]{1,0:T(1,128)}) custom-call(f32[1,128]{1,0:T(1,128)S(1)} %get-tuple-element.7.reg_row, f32[2,2,128,128]{3,2,1,0:T(8,128)S(1)} %get-tuple-element.8.sums, f32[1,128]{1,0:T(1,128)S(1)} %get-tuple-element.9.leaf_row), custom_call_target="tpu_custom_call" | custom-call | tf_op jit(solution)/shard_map/gains/pallas_call | solution.py:327

commit v6 on v5

--- a/solution.py
+++ b/solution.py
@@ -22,7 +22,8 @@
 
 
 def split3(value):
-    first = value.astype(jnp.bfloat16)
+    largest = float(jnp.finfo(jnp.bfloat16).max)
+    first = jnp.clip(value, -largest, largest).astype(jnp.bfloat16)
     rest = value - first.astype(jnp.float32)
     second = rest.astype(jnp.bfloat16)
     third = (rest - second.astype(jnp.float32)).astype(jnp.bfloat16)
@@ -70,10 +71,18 @@
     return leaf
 
 
-def exchange_kernel(bin_hbm, grad_hbm, hess_hbm, feat_hbm, thr_hbm, reg_hbm, sums, leaf_row, reg_row,
+def exchange_kernel(*refs):
+    dma, regular = pltpu.SemaphoreType.DMA, pltpu.SemaphoreType.REGULAR
+    pl.run_scoped(
+        lambda *own: exchange(*refs, *own),
+        regular((len(RANK_GROUPS),)), regular, regular, regular, regular,
+        dma((2,)), dma, dma((ND,)), dma((6,)), dma, dma, dma)
+
+
+def exchange(bin_hbm, grad_hbm, hess_hbm, feat_hbm, thr_hbm, reg_hbm, sums, leaf_row, reg_row,
                     leaf_sums, values, parcels, rows, columns, leaves, below, own_bins, own_grad, own_hess, reg_in, feat_in, thr_in, feat_tbl, thr_tbl,
-                    local_sem, ready, gathered, everyone, earlier_ok, later_ok,
-                    block_send, block_recv, data_send, data_recv, leaf_send, leaf_recv):
+                    ready, gathered, everyone, earlier_ok, later_ok, block_recv, data_recv, leaf_recv,
+                    local_sem, block_send, data_send, leaf_send):
     f, d = lax.axis_index('feat'), lax.axis_index('data')
     x, core = d // 2, d % 2
     chief, other = 2 * x + 1, 2 * x + 1 - core
@@ -251,7 +260,11 @@
     pltpu.make_async_copy(arrived, arrived, data_send).wait()
 
 
-def gain_kernel(reg_row, sums, leaf_row, gain_hbm, leaf_hbm, heap, gains, out_sem):
+def gain_kernel(*refs):
+    pl.run_scoped(lambda out_sem: fill_gains(*refs, out_sem), pltpu.SemaphoreType.DMA((2,)))
+
+
+def fill_gains(reg_row, sums, leaf_row, gain_hbm, leaf_hbm, heap, gains, out_sem):
     reg = reg_row[...]
 
     def score(g, h):
@@ -291,7 +304,6 @@
     def per_device(binned, gradient, hessian, split_feat, split_thr, reg_lambda):
         hbm = pl.BlockSpec(memory_space=pltpu.HBM)
         vmem = pl.BlockSpec(memory_space=pltpu.VMEM)
-        dma, regular = pltpu.SemaphoreType.DMA, pltpu.SemaphoreType.REGULAR
         inputs = [binned.T, gradient.reshape(1, CHUNK), hessian.reshape(1, CHUNK), split_feat, split_thr]
         sums, leaf_row, reg_row = pl.pallas_call(
             exchange_kernel,
@@ -318,8 +330,6 @@
                 pltpu.VMEM((7, 64), jnp.int32),
                 pltpu.VMEM((8, 128), jnp.int32),
                 pltpu.VMEM((8, 128), jnp.int32),
-                dma((6,)), regular((len(RANK_GROUPS),)), regular, regular, regular, regular,
-                dma, dma((2,)), dma, dma, dma, dma((ND,)),
             ],
             compiler_params=pltpu.CompilerParams(collective_id=0, has_side_effects=True, vmem_limit_bytes=24 * 2 ** 20),
             name='exchange',
@@ -335,7 +345,6 @@
             scratch_shapes=[
                 pltpu.VMEM((2, 2, LEAVES, 128), jnp.float32),
                 pltpu.VMEM((255, 1, 255), jnp.float32),
-                dma((2,)),
             ],
             compiler_params=pltpu.CompilerParams(vmem_limit_bytes=24 * 2 ** 20),
             name='gains',

time: 17.6 us -> 17.3 us (0.983)
  Pallas kernels: 16.1 us -> 15.9 us
    pallas_call x1, Pallas kernels: 15.1 us -> 14.9 us  [per_device(): pl.pallas_call(exchange_kernel, out_shape=[jax.ShapeDtypeStruct((2, 2, LE...]
where the time goes in v6:
time: 17.3 us; the launch traced here: 17.2 us
  Pallas kernels  15.9 us (92%)
  between operations  1.29 us (7%)
    pallas_call x1, Pallas kernels, per_device(): pl.pallas_call(exchange_kernel, out_shape=[jax.ShapeDtypeStruct((2, 2, LE...  14.9 us
    pallas_call x1, Pallas kernels, per_device(): pl.pallas_call(gain_kernel, out_shape=[jax.ShapeDtypeStruct((255, 1, 255)...  0.98 us

profile of v6, /device:TPU:1, one launch (start us, length us, event | category | flops | bytes accessed | tf_op | source)
XLA Modules:
  0.0 17.2 jit_solution(9660843649497241715)
XLA Ops:
  1.3 14.9 %exchange.1 = (f32[2,2,128,128]{3,2,1,0:T(8,128)S(1)}, f32[1,128]{1,0:T(1,128)S(1)}, f32[1,128]{1,0:T(1,128)S(1)}) custom-call(s32[8,512]{1,0:T(8,128)} %bitcast.4, f32[1,512]{1,0:T(1,128)} %bitcast.5, f32[1,512]{1,0:T(1,128)} %bitcast.6, s32[7,64]{1,0:T(8,128)} %refs_3_.1, s32[7,64]{1,0:T(8,128)} %refs_4_.1, f32[1]{0:T(128)S(6)} %copy.8.refs_5_), custom_call_target="tpu_custom_call" | custom-call | tf_op jit(solution)/shard_map/exchange/pallas_call | solution.py:308
  16.2 1.0 %gains.1 = (f32[255,1,255]{2,1,0:T(1,128)}, f32[1,128]{1,0:T(1,128)}) custom-call(f32[1,128]{1,0:T(1,128)S(1)} %get-tuple-element.7.refs_0_, f32[2,2,128,128]{3,2,1,0:T(8,128)S(1)} %get-tuple-element.8.refs_1_, f32[1,128]{1,0:T(1,128)S(1)} %get-tuple-element.9.refs_2_), custom_call_target="tpu_custom_call" | custom-call | tf_op jit(solution)/shard_map/gains/pallas_call | solution.py:337

commit v7 on v6

--- a/solution.py
+++ b/solution.py
@@ -216,10 +216,27 @@
     def build(k):
         below[k] = jnp.where(columns[:, k:k + 1] <= iota((CHUNK, NBINS), 1).astype(jnp.float32), jnp.float32(1), zero).astype(jnp.bfloat16)
 
+    def finish_sends():
+        @pl.when(is_chief)
+        def _():
+            sent = values.at[0, pl.ds(0, NF - 1)]
+            pltpu.make_async_copy(sent, sent, block_send).wait()
+            told = leaves.at[pl.ds(0, ND - 1)]
+            pltpu.make_async_copy(told, told, leaf_send).wait()
+            pltpu.make_async_copy(told, told, leaf_send).wait()
+
+        @pl.when(jnp.logical_not(is_chief))
+        def _():
+            sent = values.at[0]
+            pltpu.make_async_copy(sent, sent, block_send).wait()
+        pltpu.make_async_copy(arrived, arrived, data_send).wait()
+
     totals = [None, None]
     for k, s in enumerate(sources):
         for later in BUILD.get(k, ()):
             build(later)
+        if k == ND - 1:
+            finish_sends()
         arrival = pltpu.make_async_copy(leaves.at[s], leaves.at[s], leaf_recv.at[s])
         if k < 2:
             pl.when(jnp.logical_not(is_chief))(arrival.wait)
@@ -244,20 +261,6 @@
     for part in range(2):
         for half in range(2):
             sums[part, half] = totals[part][:, 128 * half:128 * (half + 1)]
-
-    @pl.when(is_chief)
-    def _():
-        sent = values.at[0, pl.ds(0, NF - 1)]
-        pltpu.make_async_copy(sent, sent, block_send).wait()
-        told = leaves.at[pl.ds(0, ND - 1)]
-        pltpu.make_async_copy(told, told, leaf_send).wait()
-        pltpu.make_async_copy(told, told, leaf_send).wait()
-
-    @pl.when(jnp.logical_not(is_chief))
-    def _():
-        sent = values.at[0]
-        pltpu.make_async_copy(sent, sent, block_send).wait()
-    pltpu.make_async_copy(arrived, arrived, data_send).wait()
 
 
 def gain_kernel(*refs):

time: 17.3 us -> 17.3 us (level)
  no operation moved by 1% of the time
where the time goes in v7:
time: 17.3 us; the launch traced here: 17.2 us
  Pallas kernels  15.9 us (92%)
  between operations  1.28 us (7%)
    pallas_call x1, Pallas kernels, per_device(): pl.pallas_call(exchange_kernel, out_shape=[jax.ShapeDtypeStruct((2, 2, LE...  14.9 us
    pallas_call x1, Pallas kernels, per_device(): pl.pallas_call(gain_kernel, out_shape=[jax.ShapeDtypeStruct((255, 1, 255)...  0.98 us

profile of v7, /device:TPU:1, one launch (start us, length us, event | category | flops | bytes accessed | tf_op | source)
XLA Modules:
  0.0 17.2 jit_solution(232100760198871755)
XLA Ops:
  1.3 14.9 %exchange.1 = (f32[2,2,128,128]{3,2,1,0:T(8,128)S(1)}, f32[1,128]{1,0:T(1,128)S(1)}, f32[1,128]{1,0:T(1,128)S(1)}) custom-call(s32[8,512]{1,0:T(8,128)} %bitcast.4, f32[1,512]{1,0:T(1,128)} %bitcast.5, f32[1,512]{1,0:T(1,128)} %bitcast.6, s32[7,64]{1,0:T(8,128)} %refs_3_.1, s32[7,64]{1,0:T(8,128)} %refs_4_.1, f32[1]{0:T(128)S(6)} %copy.8.refs_5_), custom_call_target="tpu_custom_call" | custom-call | tf_op jit(solution)/shard_map/exchange/pallas_call | solution.py:311
  16.2 1.0 %gains.1 = (f32[255,1,255]{2,1,0:T(1,128)}, f32[1,128]{1,0:T(1,128)}) custom-call(f32[1,128]{1,0:T(1,128)S(1)} %get-tuple-element.7.refs_0_, f32[2,2,128,128]{3,2,1,0:T(8,128)S(1)} %get-tuple-element.8.refs_1_, f32[1,128]{1,0:T(1,128)S(1)} %get-tuple-element.9.refs_2_), custom_call_target="tpu_custom_call" | custom-call | tf_op jit(solution)/shard_map/gains/pallas_call | solution.py:340

commit v8 on v7

--- a/solution.py
+++ b/solution.py
@@ -12,10 +12,11 @@
 CHUNK = 512
 LEAVES = 128
 HUB = 0
-FEAT_ORDER = (0, 1, 2, 4, 3, 8, 9, 7, 5, 12, 6, 10, 11, 14, 13, 15)
+LATER_ORDER = (4, 3, 8, 7, 1, 12, 5, 0, 6, 10, 9, 11, 13, 15, 2, 14)
+FEAT_ORDER = (0, 1, 2, 4, 3, 8, 7, 5, 12, 6, 10, 9, 11, 14, 13, 15)
 FEAT_RANK = [FEAT_ORDER.index(f) for f in range(NF)]
 BUILD = {0: (0,), 1: (1,), 2: (2, 3), 3: (4, 5, 6, 7)}
-SEND_ORDER = (0, 8, 15, 3, 2, 13, 4, 1, 5, 14, 7, 9, 11, 6, 12, 10)
+SEND_ORDER = (0, 8, 3, 9, 4, 1, 11, 7, 12, 13, 5, 6, 14, 10, 2, 15)
 RANK_GROUPS = ((0, 7), (8, 15))
 DATA_ORDER = (1, 0, 3, 2, 5, 4, 7, 6)
 MESH = pl.DeviceIdType.MESH
@@ -176,13 +177,13 @@
         def _():
             pl.semaphore_wait(ready.at[group], count)
             signal(later_ok, data=other)
-            for peer in FEAT_ORDER[first:last + 1]:
+            for peer in [p for p in LATER_ORDER if first <= FEAT_RANK[p] <= last]:
                 pl.when(FEAT_RANK[peer] > rank)(lambda: send_block(peer, 1))
 
         @pl.when(jnp.logical_not(is_chief) & (count > 0))
         def _():
             pl.semaphore_wait(later_ok, 1)
-            for peer in FEAT_ORDER[first:last + 1]:
+            for peer in [p for p in LATER_ORDER if first <= FEAT_RANK[p] <= last]:
                 pl.when(FEAT_RANK[peer] > rank)(lambda: send_block(peer, 0))
 
     reg_row[...] = jnp.broadcast_to(reg_in[0], (1, 128))

time: 17.3 us -> 17.3 us (level)
  no operation moved by 1% of the time
where the time goes in v8:
time: 17.3 us; the launch traced here: 17.1 us
  Pallas kernels  15.9 us (92%)
  between operations  1.28 us (7%)
    pallas_call x1, Pallas kernels, per_device(): pl.pallas_call(exchange_kernel, out_shape=[jax.ShapeDtypeStruct((2, 2, LE...  14.9 us
    pallas_call x1, Pallas kernels, per_device(): pl.pallas_call(gain_kernel, out_shape=[jax.ShapeDtypeStruct((255, 1, 255)...  0.98 us

profile of v8, /device:TPU:1, one launch (start us, length us, event | category | flops | bytes accessed | tf_op | source)
XLA Modules:
  0.0 17.1 jit_solution(18092243526747624759)
XLA Ops:
  1.3 14.9 %exchange.1 = (f32[2,2,128,128]{3,2,1,0:T(8,128)S(1)}, f32[1,128]{1,0:T(1,128)S(1)}, f32[1,128]{1,0:T(1,128)S(1)}) custom-call(s32[8,512]{1,0:T(8,128)} %bitcast.4, f32[1,512]{1,0:T(1,128)} %bitcast.5, f32[1,512]{1,0:T(1,128)} %bitcast.6, s32[7,64]{1,0:T(8,128)} %refs_3_.1, s32[7,64]{1,0:T(8,128)} %refs_4_.1, f32[1]{0:T(128)S(6)} %copy.8.refs_5_), custom_call_target="tpu_custom_call" | custom-call | tf_op jit(solution)/shard_map/exchange/pallas_call | solution.py:312
  16.2 1.0 %gains.1 = (f32[255,1,255]{2,1,0:T(1,128)}, f32[1,128]{1,0:T(1,128)}) custom-call(f32[1,128]{1,0:T(1,128)S(1)} %get-tuple-element.7.refs_0_, f32[2,2,128,128]{3,2,1,0:T(8,128)S(1)} %get-tuple-element.8.refs_1_, f32[1,128]{1,0:T(1,128)S(1)} %get-tuple-element.9.refs_2_), custom_call_target="tpu_custom_call" | custom-call | tf_op jit(solution)/shard_map/gains/pallas_call | solution.py:341
